TPU v7x, 256 devices: a whole 4x4x8 slice. The times are simulated.
256 devices in a mesh: lb: 8 (over y, core), rb: 8 (over z), wa: 4 (over x).
Axes of the slice: x: 4, y: 4, z: 8, core: 2. Of those that a mesh axis runs over, the one named last changes fastest.
Arguments:
- state: bfloat16 [4, 4, 4, 1024, 1024], P('wa', None, None, 'lb', 'rb'), may hold values from -14 to 14
- left_env: bfloat16 [3, 4, 1024, 4, 1024], P(None, None, 'lb', 'wa'), may hold values from -1 to 2.5
- right_env: bfloat16 [3, 4, 1024, 4, 1024], P(None, None, 'rb', 'wa'), may hold values from -1 to 2.5
- site_one: float32 [3, 3, 2, 2], replicated, may hold values from -2 to 3
- site_two: float32 [3, 3, 2, 2], replicated, may hold values from -2 to 3
Outputs:
- next_vector: float32 [4, 4, 4, 1024, 1024], P('wa', None, None, 'lb', 'rb')
- coefficients: float32 [2], replicated
All inputs are finite; a program needn't handle non-finite values.
Results may differ from a plain program's by a relative error of at most 0.02.
Values may be sent and summed in bfloat16 or wider, within the bound.
A program may use at most 128 MiB of HBM per device.

v0:
```python
import functools

import jax
import jax.numpy as jnp
from jax import lax
from jax.sharding import Mesh
from jax.sharding import PartitionSpec as P

LB = ("lb_0", "lb_1")
LB_RB_WA = ("lb_0", "lb_1", "rb", "wa")


EPSILON = 1e-06


def in_order(tiles, dim):
    tiles = jnp.moveaxis(tiles, 0, dim)
    shape = tiles.shape
    return tiles.reshape(*shape[:dim], shape[dim] * shape[dim + 1], *shape[dim + 2 :])


def sent_to_all(x, axis):
    copies = jnp.broadcast_to(x, (lax.axis_size(axis), *x.shape))
    return lax.all_to_all(copies, axis, split_axis=0, concat_axis=0, tiled=True)


def gather_directly(x, axis, dim):
    return in_order(sent_to_all(x, axis), dim)


def piecewise(x, axis, dim, apply, out_dim):
    peers, rows = (lax.axis_size(axis), x.shape[dim])
    count = 2 if rows % 2 == 0 else 1
    outs, length = ([], rows // count)
    for k in range(count):
        piece = lax.slice_in_dim(x, k * length, (k + 1) * length, axis=dim)
        starts = jnp.arange(peers) * rows + k * length
        outs.append(jax.vmap(apply)(lax.all_gather(piece, axis), starts))
    return in_order(jnp.concatenate(outs, axis=out_dim + 1), out_dim)


def over_axes(x, axes):
    return functools.reduce(lax.psum, axes, x)


def pair_tensor(site_one, site_two):
    joined = jnp.einsum("wuac,uvbd->wvabcd", site_one, site_two)
    mpo_width = site_one.shape[0]
    states = site_one.shape[2] * site_two.shape[2]
    return joined.reshape(mpo_width, mpo_width, states, states)


def body(state, left_env, right_env, site_one, site_two):
    mpo_pair = pair_tensor(site_one, site_two)
    entries = float(state.size * lax.axis_size(LB) * lax.axis_size("rb") * lax.axis_size("wa"))
    state_values = state.astype(jnp.float32)
    blocks = gather_directly(state, "wa", 0)
    left_sum = lax.psum_scatter(
        jnp.einsum(
            "wgmcp,ghsmn->pcwhsn", left_env, blocks, preferred_element_type=jnp.float32
        ).astype(jnp.bfloat16),
        LB,
        scatter_dimension=0,
        tiled=True,
    ).astype(jnp.float32)
    mixed_state = jnp.einsum("pcwhsn,wvst->pcvhtn", left_sum, mpo_pair).astype(jnp.bfloat16)

    def right_term(shard_piece, first_row):
        return jnp.einsum(
            "pcvhtn,vhndq->cdtpq", shard_piece, right_env, preferred_element_type=jnp.float32
        )

    image_terms = piecewise(mixed_state, "wa", 1, right_term, 0)
    image_part = lax.psum_scatter(
        image_terms.astype(jnp.bfloat16), "rb", scatter_dimension=4, tiled=True
    ).astype(jnp.float32)
    applied = lax.all_to_all(
        image_part.astype(jnp.bfloat16), "wa", split_axis=0, concat_axis=1, tiled=True
    ).astype(image_part.dtype)
    squares, crossed, image_squares = (
        over_axes(jnp.sum(state_values * state_values), LB_RB_WA),
        over_axes(jnp.sum(state_values * applied), LB_RB_WA),
        over_axes(jnp.sum(applied * applied), LB_RB_WA),
    )
    norm_sq = squares / entries + EPSILON
    projection = crossed / entries
    alpha_coef = projection / norm_sq
    residual = (applied - alpha_coef * state_values) / jnp.sqrt(norm_sq)
    beta_coef = jnp.sqrt((image_squares / entries - alpha_coef * projection) / norm_sq + EPSILON)
    next_vector = residual / beta_coef
    return (next_vector, jnp.stack([alpha_coef, beta_coef]))


def solution(mesh):
    torus = Mesh(
        mesh.devices.reshape(4, 2, mesh.shape["rb"], mesh.shape["wa"]), ("lb_0", "lb_1", "rb", "wa")
    )
    in_specs = (
        P("wa", None, None, LB, "rb"),
        P(None, None, LB, "wa", None),
        P(None, None, "rb", "wa", None),
        P(),
        P(),
    )
    out_specs = (P("wa", None, None, LB, "rb"), P())
    return jax.shard_map(body, mesh=torus, in_specs=in_specs, out_specs=out_specs, check_vma=False)
```

profile of v0, /device:TPU:1, one launch (start us, length us, event | category | flops | bytes accessed | tf_op | source)
XLA Modules:
  0.0 417.5 jit_solution(14569673637582960244)
XLA Ops:
  7.2 0.0 copy-start
  7.2 0.0 reduce-scatter.7.cloned.1.call-start
  7.2 2.2 copy.24
  9.4 1.5 broadcast_in_dim.3
  11.0 30.0 %all_to_all.14 = bf16[4,1,4,4,128,128]{4,5,3,2,1,0:T(8,128)(2,1)S(1)} all-to-all(bf16[4,1,4,4,128,128]{4,5,3,2,1,0:T(8,128)(2,1)S(1)} %broadcast_in_dim.3), channel_id=1, replica_groups=mesh['lb_0'=4,'lb_1'=2,'rb'=8,'wa'=4] {'wa'}, dimensions={0} | all-to-all | bytes 4194304 | tf_op jit(solution)/shard_map/all_to_all | solution.py:24
  41.0 0.0 copy-done
  41.0 9.1 %fusion = bf16[1024,1,3,4,4,128]{0,5,2,4,3,1:T(8,128)(2,1)} fusion(bf16[3,4,128,1,1024]{4,2,3,1,0:T(8,128)(2,1)S(1)} %copy-done, bf16[4,1,4,4,128,128]{4,5,3,2,1,0:T(8,128)(2,1)S(1)} %all_to_all.14), kind=kOutput, calls=%fused_computation.1 | convolution fusion | flops 6448742400 | bytes 17825792 | tf_op jit(solution)/shard_map/wgmcp,ghsmn->pcwhsn/dot_general | solution.py:59
  50.1 27.1 %copy.48 = bf16[1024,1,3,4,4,128]{5,2,4,3,1,0:T(4,128)(2,1)} copy(bf16[1024,1,3,4,4,128]{0,5,2,4,3,1:T(8,128)(2,1)} %fusion) | data formatting | bytes 25165824
  77.2 31.8 %reshape.89 = bf16[1024,6144]{1,0:T(8,128)(2,1)} reshape(bf16[1024,1,4,4,3,128]{5,4,3,2,1,0:T(4,128)(2,1)} %bitcast.81) | data formatting | bytes 25165824
  109.1 0.0 copy-start.3
  109.1 0.0 copy-start.4
  109.1 0.0 reduce-scatter.7.cloned.1.call-update
  109.1 0.0 all-gather.3.cloned.1.call-start
  109.1 0.6 copy-done.3
  109.8 0.0 copy-done.4
  109.8 0.2 convolution_bitcast_fusion
  109.9 0.2 copy.23
  110.2 0.2 copy.36
  110.4 75.7 %reduce-scatter.7.cloned.1.call-done = bf16[128,6144]{1,0:T(8,128)(2,1)} async-done(((bf16[1024,6144]{1,0:T(8,128)(2,1)}), bf16[128,6144]{1,0:T(8,128)(2,1)}) %reduce-scatter.7.cloned.1.call-update) | async-done | bytes 1572880
  186.0 4.6 %reshape.90 = bf16[128,1,4,4,3,128]{5,4,3,2,1,0:T(4,128)(2,1)S(1)} reshape(bf16[128,6144]{1,0:T(8,128)(2,1)} %reduce-scatter.7.cloned.1.call-done) | data formatting | bytes 3145728
  190.6 2.7 copy.49
  193.3 3.3 copy.27
  196.6 3.1 fusion.13
  199.7 0.0 all-gather.3.cloned.1.call-update
  199.7 0.0 reduce-scatter.9.cloned.1.call-start
  199.8 68.3 %all-gather.3.cloned.1.call-done = bf16[512,1,3,4,4,128]{5,4,3,0,2,1:T(4,128)(2,1)} async-done(((bf16[128,1,3,4,4,128]{5,4,3,0,2,1:T(4,128)(2,1)}), bf16[512,1,3,4,4,128]{5,4,3,0,2,1:T(4,128)(2,1)}) %all-gather.3.cloned.1.call-update) | async-done | bytes 6291472 | tf_op jit(solution)/shard_map/all_gather | solution.py:38
  268.0 10.6 %fusion.3 = bf16[4,1,4,128,1024]{4,3,2,0,1:T(8,128)(2,1)} fusion(bf16[4,128,3,4,4,128]{5,4,3,1,0,2:T(4,128)(2,1)} %bitcast.91, bf16[3,4,128,1,1024]{4,2,3,1,0:T(8,128)(2,1)} %param.7), kind=kOutput, calls=%fused_computation.5 | convolution fusion | flops 6444548096 | bytes 13631488 | tf_op jit(solution)/shard_map/vmap(pcvhtn,vhndq->cdtpq)/dot_general | solution.py:69
  278.6 7.8 %copy.50 = bf16[4,1,4,128,1024]{3,2,0,1,4:T(4,128)(2,1)} copy(bf16[4,1,4,128,1024]{4,3,2,0,1:T(8,128)(2,1)} %fusion.3) | data formatting | bytes 8388608
  286.5 7.8 %reshape.91 = bf16[1024,2048]{1,0:T(8,128)(2,1)} reshape(bf16[1024,1,4,4,128]{4,3,2,1,0:T(4,128)(2,1)} %bitcast.82) | data formatting | bytes 8388608
  294.3 0.0 reduce-scatter.9.cloned.1.call-update
  294.3 0.0 copy-start.1
  294.3 56.3 %reduce-scatter.9.cloned.1.call-done = bf16[128,2048]{1,0:T(8,128)(2,1)} async-done(((bf16[1024,2048]{1,0:T(8,128)(2,1)}), bf16[128,2048]{1,0:T(8,128)(2,1)}) %reduce-scatter.9.cloned.1.call-update) | async-done | bytes 524304
  350.6 2.2 reshape.92
  352.8 2.2 copy.51
  355.0 12.5 %all_to_all.15 = bf16[4,1,4,128,128]{4,3,2,1,0:T(8,128)(2,1)S(1)} all-to-all(bf16[4,1,4,128,128]{4,3,2,1,0:T(8,128)(2,1)} %bitcast.87), channel_id=1, replica_groups=mesh['lb_0'=4,'lb_1'=2,'rb'=8,'wa'=4] {'wa'}, dimensions={0} | all-to-all | bytes 1048576 | tf_op jit(solution)/shard_map/all_to_all | solution.py:77
  367.5 0.0 copy-start.2
  367.5 0.8 copy-done.2
  368.3 1.9 fusion.17
  370.2 9.2 %all-reduce.2 = (f32[]{:T(128)}, f32[]{:T(128)}, f32[]{:T(128)}) all-reduce(f32[]{:T(128)} %get-tuple-element.4, f32[]{:T(128)} %get-tuple-element.3, f32[]{:T(128)} %get-tuple-element.2), channel_id=1, replica_groups=mesh['lb_0'=4,'lb_1'=2,'rb'=8,'wa'=4] {'lb_0'}, use_global_device_ids=true, to_apply=%region_8.0 | all-reduce | flops 3 | bytes 24 | tf_op jit(solution)/shard_map/psum | solution.py:43
  379.4 6.6 %all-reduce.3 = (f32[]{:T(128)}, f32[]{:T(128)}, f32[]{:T(128)}) all-reduce(f32[]{:T(128)} %get-tuple-element.11, f32[]{:T(128)} %get-tuple-element.12, f32[]{:T(128)} %get-tuple-element.13), channel_id=1, replica_groups=mesh['lb_0'=4,'lb_1'=2,'rb'=8,'wa'=4] {'lb_1'}, use_global_device_ids=true, to_apply=%region_9.0 | all-reduce | flops 3 | bytes 24 | tf_op jit(solution)/shard_map/psum | solution.py:43
  386.0 12.5 %all-reduce = (f32[]{:T(128)}, f32[]{:T(128)}, f32[]{:T(128)}) all-reduce(f32[]{:T(128)} %get-tuple-element.14, f32[]{:T(128)} %get-tuple-element.15, f32[]{:T(128)} %get-tuple-element.16), channel_id=1, replica_groups=mesh['lb_0'=4,'lb_1'=2,'rb'=8,'wa'=4] {'rb'}, use_global_device_ids=true, to_apply=%region_10.0 | all-reduce | flops 3 | bytes 24 | tf_op jit(solution)/shard_map/psum | solution.py:43
  398.5 7.5 %all-reduce.1 = (f32[]{:T(128)}, f32[]{:T(128)}, f32[]{:T(128)}) all-reduce(f32[]{:T(128)} %get-tuple-element.5, f32[]{:T(128)} %get-tuple-element.6, f32[]{:T(128)} %get-tuple-element.7), channel_id=1, replica_groups=mesh['lb_0'=4,'lb_1'=2,'rb'=8,'wa'=4] {'wa'}, use_global_device_ids=true, to_apply=%region_11.0 | all-reduce | flops 3 | bytes 24 | tf_op jit(solution)/shard_map/psum | solution.py:43
  408.0 0.6 pad_maximum_fusion
  408.6 2.3 fusion.18
  410.9 0.0 copy-done.1
Async XLA Ops:
  7.2 33.8 %copy-start = (bf16[3,4,128,1,1024]{4,2,3,1,0:T(8,128)(2,1)S(1)}, bf16[3,4,128,1,1024]{4,2,3,1,0:T(8,128)(2,1)}, u32[]{:S(2)}) copy-start(bf16[3,4,128,1,1024]{4,2,3,1,0:T(8,128)(2,1)} %param.6) | copy-start | bytes 9437188
  7.2 178.8 %reduce-scatter.7.cloned.1.call-start = ((), (), s32[]{:S(2)}) async-start(), calls=%async_computation.5 | async-start | bytes 14155776
  109.1 0.7 copy-start.3
  109.1 0.7 copy-start.4
  109.1 158.9 %all-gather.3.cloned.1.call-start = ((), (), s32[]{:S(2)}) async-start(), calls=%async_computation.4 | async-start | bytes 7864320 | tf_op jit(solution)/shard_map/all_gather | solution.py:38
  199.7 150.9 %reduce-scatter.9.cloned.1.call-start = ((), (), s32[]{:S(2)}) async-start(), calls=%async_computation.6 | async-start | bytes 4718592
  294.3 116.6 %copy-start.1 = (bf16[3,4,128,1,1024]{4,2,3,1,0:T(8,128)(2,1)S(1)}, bf16[3,4,128,1,1024]{4,2,3,1,0:T(8,128)(2,1)}, u32[]{:S(2)}) copy-start(bf16[3,4,128,1,1024]{4,2,3,1,0:T(8,128)(2,1)} %param.6) | copy-start | bytes 9437188
  367.5 0.8 copy-start.2
Sparse Core Ops, SparseCore 0:
  109.2 76.7 reduce-scatter.6
  199.8 68.1 all-gather.2
  294.4 56.1 reduce-scatter.8
where the time goes:
time: 424 us; the launch traced here: 417 us
  waiting for transfers between devices  200 us (47%)
  local copies, waits for them, and re-layouts  95.2 us (22%)
  blocking collectives  78.3 us (18%)
  matrix products  23 us (5%)
  between operations  15.8 us (4%)
  other arithmetic  4.85 us (1%)
    unnamed x5, waiting for transfers between devices  132 us
    unnamed x18, local copies, waits for them, and re-layouts  87.8 us
    all_gather x1, waiting for transfers between devices, piecewise(): outs.append(jax.vmap(apply)(lax.all_gather(piece, axis), starts))  68.3 us
    psum x4, blocking collectives, over_axes(): return functools.reduce(lax.psum, axes, x)  35.7 us
    all_to_all x1, blocking collectives, sent_to_all(): return lax.all_to_all(copies, axis, split_axis=0, concat_axis=0, tiled=True)  30 us
    all_to_all x1, blocking collectives, body(): lax.all_to_all(image_part.astype(jnp.bfloat16), 'wa', split_axis=0, conca...  12.5 us
    dot_general x1, matrix products, right_term(): jnp.einsum('pcvhtn,vhndq->cdtpq', shard_piece, right_env, preferred_eleme...  10.6 us
    dot_general x1, matrix products, body(): jnp.einsum('wgmcp,ghsmn->pcwhsn', left_env, blocks, preferred_element_typ...  9.1 us
  transfers between devices with their start and end apart: 3, of which 3 were waited for; matrix products, arithmetic and copies ran while one was open for 0% of the time, Pallas kernels for 0%

commit v1 on v0

v1 whole, which is shorter than its diff:
```python
import functools

import jax
import jax.numpy as jnp
from jax import lax
from jax.experimental import pallas as pl
from jax.experimental.pallas import tpu as pltpu
from jax.sharding import Mesh
from jax.sharding import PartitionSpec as P

LB = ("lb_0", "lb_1")
EPSILON = 1e-06
ENTRIES = 4.0 * 4 * 4 * 1024 * 1024
F32, BF16 = jnp.float32, jnp.bfloat16
X, Y, Z, H = 4, 4, 8, 4
N_SEMS = 160
UNITS = (0, 1, 3, 2)


def pair_tensor(site_one, site_two):
    one = site_one[:, :, None, :, None, :, None]
    two = site_two[None, :, :, None, :, None, :]
    return jnp.sum(one * two, axis=1).reshape(144)


def matmul(a, b):
    return lax.dot_general(a, b, (((1,), (0,)), ((), ())), preferred_element_type=F32)


def kernel(
    mpo,
    state,
    left,
    right,
    out,
    coef,
    blocks,
    left_other,
    left_t,
    far,
    up,
    down,
    up_far,
    down_far,
    from_below,
    from_above,
    left_sum,
    mixed,
    envs,
    image,
    ring_half,
    ring_full,
    sums_z,
    sums_y,
    sums_x,
    send_sems,
    recv_sems,
    local_sems,
):
    y, c, z, x = (lax.axis_index(a) for a in ("lb_0", "lb_1", "rb", "wa"))
    other = 1 - c

    def at(dx=0, dy=0, dz=0, core=None):
        return (
            lax.rem(y + dy, Y),
            c if core is None else core,
            lax.rem(z + dz, Z),
            lax.rem(x + dx, X),
        )

    used = []

    def copy(src, dst, device):
        k = len(used)
        used.append(
            pltpu.make_async_remote_copy(
                src_ref=src,
                dst_ref=dst,
                send_sem=send_sems.at[k],
                recv_sem=recv_sems.at[k],
                device_id=device,
                device_id_type=pl.DeviceIdType.MESH,
            )
        )
        return used[-1]

    partner = at(core=other)
    x_up, x_down = at(dx=1), at(dx=X - 1)
    y_up, y_down = at(dy=1), at(dy=Y - 1)
    z_up, z_down = at(dz=1), at(dz=Z - 1)
    z_peers = [at(dz=k) for k in range(1, Z)]
    y_peers = [partner] + [at(dy=k, core=core) for k in range(1, Y) for core in (c, other)]
    x_peers = [at(dx=k) for k in range(1, X)]

    barrier = pltpu.get_barrier_semaphore()
    peers = z_peers + y_peers + x_peers
    for peer in peers:
        pl.semaphore_signal(barrier, inc=1, device_id=peer, device_id_type=pl.DeviceIdType.MESH)

    own = x * 2 + c
    local = [
        pltpu.make_async_copy(state.at[h], blocks.at[h, own], local_sems.at[h]) for h in range(H)
    ]
    local.append(pltpu.make_async_copy(right, envs.at[0], local_sems.at[H]))
    for item in local:
        item.start()
    pl.semaphore_wait(barrier, len(peers))

    g_below = lax.rem(x + X - 1, X) * 2 + c
    g_above = lax.rem(x + 1, X) * 2 + c
    g_far = lax.rem(x + 2, X) * 2 + c
    lo, hi = pl.ds(0, 64), pl.ds(64, 64)
    b_up = [copy(state.at[h], blocks.at[h, own], x_up) for h in range(H)]
    b_down = [copy(state.at[h], blocks.at[h, own], x_down) for h in range(H)]
    b_own = [copy(state.at[h], blocks.at[h, own], partner) for h in range(H)]
    bf_up = [copy(blocks.at[h, g_below, lo], blocks.at[h, g_below, lo], x_up) for h in range(H)]
    bf_down = [copy(blocks.at[h, g_above, hi], blocks.at[h, g_above, hi], x_down) for h in range(H)]
    b_pass = [
        [
            copy(blocks.at[h, g_below], blocks.at[h, g_below], partner),
            copy(blocks.at[h, g_above], blocks.at[h, g_above], partner),
            copy(blocks.at[h, g_far, lo], blocks.at[h, g_far, lo], partner),
            copy(blocks.at[h, g_far, hi], blocks.at[h, g_far, hi], partner),
        ]
        for h in range(H)
    ]

    def start_own(h):
        b_up[h].start()
        b_down[h].start()
        b_own[h].start()

    def pass_near(h):
        b_up[h].wait_recv()
        bf_up[h].start()
        b_pass[h][0].start()
        b_down[h].wait_recv()
        bf_down[h].start()
        b_pass[h][1].start()

    def get_blocks(h):
        bf_up[h].wait_recv()
        b_pass[h][2].start()
        bf_down[h].wait_recv()
        b_pass[h][3].start()
        local[h].wait()
        b_own[h].wait_recv()
        for item in b_pass[h]:
            item.wait_recv()

    a_swap = [
        copy(
            left.at[:, :, pl.ds(pl.multiple_of(k * 256 + other * 128, 128), 128)],
            left_other.at[k],
            partner,
        )
        for k in range(Y)
    ]

    def transpose_own(i, _):
        w, g = i // 4, lax.rem(i, 4)
        for r in range(Y):
            cols = pl.ds(pl.multiple_of(lax.rem(y + r, Y) * 256 + c * 128, 128), 128)
            left_t[
                r,
                pl.ds(pl.multiple_of(w * 128, 128), 128),
                pl.ds(pl.multiple_of((g * 2 + c) * 128, 128), 128),
            ] = left[i, :, cols].T
        return 0

    def transpose_other(i, _):
        w, g = i // 4, lax.rem(i, 4)
        for r in range(Y):
            left_t[
                r,
                pl.ds(pl.multiple_of(w * 128, 128), 128),
                pl.ds(pl.multiple_of((g * 2 + other) * 128, 128), 128),
            ] = left_other[lax.rem(y + r, Y), i].T
        return 0

    start_own(0)
    start_own(1)
    for item in a_swap:
        item.start()
    lax.fori_loop(0, 12, transpose_own, 0)
    for item in a_swap:
        item.wait_recv()
    lax.fori_loop(0, 12, transpose_other, 0)

    top, low = pl.ds(0, 192), pl.ds(192, 192)
    c_far_up = [copy(far.at[h, top], up_far.at[h], y_up) for h in range(H)]
    c_far_down = [copy(far.at[h, low], down_far.at[h], y_down) for h in range(H)]
    c_up_low = [copy(up.at[h, low], from_below.at[h, low], y_up) for h in range(H)]
    c_down_top = [copy(down.at[h, top], from_above.at[h, top], y_down) for h in range(H)]
    c_up_top = [copy(up.at[h, top], from_below.at[h, top], y_up) for h in range(H)]
    c_down_low = [copy(down.at[h, low], from_above.at[h, low], y_down) for h in range(H)]

    def product(r, rows, h, store):
        def tile(j, _):
            cols = pl.ds(pl.multiple_of(j * 256, 256), 256)
            b = blocks[h, :, :, cols].reshape(1024, 256)
            store(cols, matmul(left_t[r, rows, :], b))
            return 0

        lax.fori_loop(0, 2, tile, 0)

    def start_far(h):
        def store(cols, value):
            far[h, :, cols] = value.astype(BF16)

        product(2, pl.ds(0, 384), h, store)
        c_far_up[h].start()
        c_far_down[h].start()

    def start_direct(h):
        def store_up(cols, value):
            up[h, low, cols] = value.astype(BF16)

        def store_down(cols, value):
            down[h, top, cols] = value.astype(BF16)

        product(1, low, h, store_up)
        c_up_low[h].start()
        product(3, top, h, store_down)
        c_down_top[h].start()

    def pass_far(h):
        def store_up(cols, value):
            up[h, top, cols] = (value + up_far[h, :, cols].astype(F32)).astype(BF16)

        def store_down(cols, value):
            down[h, low, cols] = (value + down_far[h, :, cols].astype(F32)).astype(BF16)

        c_far_up[h].wait_recv()
        product(1, top, h, store_up)
        c_up_top[h].start()
        c_far_down[h].wait_recv()
        product(3, low, h, store_down)
        c_down_low[h].start()

    def mix(h):
        def store(cols, value):
            left_sum[:, cols] = (
                value + from_below[h, :, cols].astype(F32) + from_above[h, :, cols].astype(F32)
            )

        for item in (c_up_low[h], c_down_top[h], c_up_top[h], c_down_low[h]):
            item.wait_recv()
        product(0, pl.ds(0, 384), h, store)

        def rows_of(i, _):
            start = pl.multiple_of(i * 16, 16)
            parts = [
                left_sum[pl.ds(w * 128 + start, 16), s * 128 : (s + 1) * 128]
                for w in range(3)
                for s in range(4)
            ]
            for v in range(3):
                for t in range(4):
                    total = None
                    for w in range(3):
                        for s in range(4):
                            term = mpo[((w * 3 + v) * 4 + s) * 4 + t] * parts[w * 4 + s]
                            total = term if total is None else total + term
                    k = v * 4 + h
                    mixed[pl.ds(t * 128 + start, 16), k * 128 : (k + 1) * 128] = total.astype(BF16)
            return 0

        lax.fori_loop(0, 8, rows_of, 0)

    half = pl.ds(c * 6, 6)
    q_lo, q_hi = pl.ds(c * 6, 3), pl.ds(c * 6 + 3, 3)
    r_up = copy(envs.at[0, half], envs.at[3, half], x_up)
    r_down = copy(envs.at[0, half], envs.at[1, half], x_down)
    rf_up = copy(envs.at[3, q_lo], envs.at[2, q_lo], x_up)
    rf_down = copy(envs.at[1, q_hi], envs.at[2, q_hi], x_down)
    rp_below = copy(envs.at[3, half], envs.at[3, half], partner)
    rp_above = copy(envs.at[1, half], envs.at[1, half], partner)
    rp_lo = copy(envs.at[2, q_lo], envs.at[2, q_lo], partner)
    rp_hi = copy(envs.at[2, q_hi], envs.at[2, q_hi], partner)

    def start_envs():
        local[H].wait()
        r_up.start()
        r_down.start()

    def pass_envs():
        r_up.wait_recv()
        rf_up.start()
        rp_below.start()
        r_down.wait_recv()
        rf_down.start()
        rp_above.start()

    def pass_far_envs():
        rf_up.wait_recv()
        rp_lo.start()
        rf_down.wait_recv()
        rp_hi.start()

    pass_near(0)
    start_own(2)
    pass_near(1)
    start_own(3)
    get_blocks(0)
    start_far(0)
    start_direct(0)
    pass_near(2)
    get_blocks(1)
    start_far(1)
    pass_far(0)
    start_direct(1)
    pass_near(3)
    get_blocks(2)
    start_far(2)
    pass_far(1)
    start_direct(2)
    mix(0)
    get_blocks(3)
    start_envs()
    start_far(3)
    pass_far(2)
    start_direct(3)
    mix(1)
    pass_far(3)
    mix(2)
    mix(3)
    pass_envs()

    def zmod(k):
        return lax.rem(z + k, Z)

    first, second = pl.ds(0, 256), pl.ds(256, 256)
    rings = []
    for u in range(4):
        ring = {}
        ring[1] = (
            copy(image.at[u, zmod(4), first], ring_half.at[u, 0], z_up),
            copy(image.at[u, zmod(4), second], ring_half.at[u, 1], z_down),
        )
        for k in (2, 3, 4):
            ring[k] = (
                copy(image.at[u, zmod(5 - k)], ring_full.at[u, 0, k - 2], z_up),
                copy(image.at[u, zmod(3 + k)], ring_full.at[u, 1, k - 2], z_down),
            )
        rings.append(ring)

    def contract(u):
        i = UNITS[u]
        if i == 1:
            rp_above.wait_recv()
        if i == 3:
            rp_below.wait_recv()
        if i == 2:
            rp_lo.wait_recv()
            rp_hi.wait_recv()

        def tile(j, _):
            cols = pl.ds(pl.multiple_of(j * 256, 256), 256)
            value = matmul(mixed[...], envs[i, :, :, cols].reshape(1536, 256)).astype(BF16)
            image[u, j * 2] = value[:, :128]
            image[u, j * 2 + 1] = value[:, 128:]
            return 0

        lax.fori_loop(0, 4, tile, 0)

    def add_into(u, k, rows, term):
        image[u, k, rows] = (image[u, k, rows].astype(F32) + term.astype(F32)).astype(BF16)

    def hop(u, k):
        for side in range(2):
            if k > 1:
                rings[u][k - 1][side].wait_recv()
                owner = zmod(5 - k) if side == 0 else zmod(3 + k)
                if k == 2:
                    add_into(u, owner, (first, second)[side], ring_half[u, side])
                else:
                    add_into(u, owner, pl.ds(0, 512), ring_full[u, side, k - 3])
            rings[u][k][side].start()

    zero = jnp.zeros((8, 128), F32)

    def folded(value):
        return jnp.sum(value.reshape(-1, 8, 128), axis=0)

    def finish(u, sums):
        rings[u][4][0].wait_recv()
        rings[u][4][1].wait_recv()
        h = lax.rem(x + UNITS[u], X)

        def piece(s, sums):
            squares, crossed, images = sums
            rows = pl.ds(pl.multiple_of(s * 128, 128), 128)
            value = (
                image[u, z, rows].astype(F32)
                + ring_full[u, 0, 2, rows].astype(F32)
                + ring_full[u, 1, 2, rows].astype(F32)
            )
            out[h, rows] = value
            start = state[h, :, rows].astype(F32)
            return (
                squares + folded(start * start),
                crossed + folded(start * value),
                images + folded(value * value),
            )

        return lax.fori_loop(0, 4, piece, sums)

    contract(0)
    hop(0, 1)
    contract(1)
    hop(1, 1)
    hop(0, 2)
    hop(1, 2)
    contract(2)
    hop(2, 1)
    hop(0, 3)
    hop(1, 3)
    hop(2, 2)
    hop(0, 4)
    pass_far_envs()
    hop(1, 4)
    contract(3)
    hop(3, 1)
    hop(2, 3)
    hop(3, 2)
    hop(2, 4)
    hop(3, 3)
    sums = finish(0, (zero, zero, zero))
    hop(3, 4)
    sums = finish(1, sums)
    sums = finish(2, sums)
    sums = finish(3, sums)

    def all_sum(values, slots, me, targets):
        slots[me] = values
        sends = [copy(slots.at[me], slots.at[me], target) for target in targets]
        for item in sends:
            item.start()
        for item in sends:
            item.wait_recv()
        return jnp.sum(slots[...], axis=0)

    packed = jnp.concatenate([jnp.sum(v, axis=0, keepdims=True) for v in sums] + [zero[:5]], axis=0)
    packed = all_sum(packed, sums_z, z, z_peers)
    packed = all_sum(packed, sums_y, y * 2 + c, y_peers)
    packed = all_sum(packed, sums_x, x, x_peers)
    means = jnp.sum(packed, axis=1, keepdims=True) * (1.0 / ENTRIES)
    square, projection, image_square = means[0:1], means[1:2], means[2:3]
    norm_sq = square + EPSILON
    alpha = projection / norm_sq
    residual_sq = (image_square - 2.0 * alpha * projection + alpha * alpha * square) / norm_sq
    beta = jnp.sqrt(residual_sq + EPSILON)
    scale = 1.0 / (jnp.sqrt(norm_sq) * beta)
    lane = lax.broadcasted_iota(jnp.int32, (8, 128), 1)
    coef[...] = jnp.where(lane == 0, alpha, beta)

    def scaled(i, _):
        h, s = i // 4, lax.rem(i, 4)
        rows = pl.ds(pl.multiple_of(s * 128, 128), 128)
        out[h, rows] = (out[h, rows] - alpha * state[h, :, rows].astype(F32)) * scale
        return 0

    lax.fori_loop(0, 16, scaled, 0)
    for item in used:
        item.wait_send()


def body(state, left_env, right_env, site_one, site_two):
    mpo = pair_tensor(site_one, site_two)
    rows = state.reshape(4, 4, 128, 128).transpose(0, 2, 1, 3).reshape(4, 128, 512)
    vmem = pl.BlockSpec(memory_space=pltpu.VMEM)
    out, coef = pl.pallas_call(
        kernel,
        out_shape=(
            jax.ShapeDtypeStruct((4, 512, 128), F32),
            jax.ShapeDtypeStruct((8, 128), F32),
        ),
        in_specs=[
            pl.BlockSpec(memory_space=pltpu.SMEM),
            vmem,
            vmem,
            pl.BlockSpec(memory_space=pl.ANY),
        ],
        out_specs=(vmem, vmem),
        scratch_shapes=[
            pltpu.VMEM((4, 8, 128, 512), BF16),
            pltpu.VMEM((4, 12, 128, 128), BF16),
            pltpu.VMEM((4, 384, 1024), BF16),
            pltpu.VMEM((4, 384, 512), BF16),
            pltpu.VMEM((4, 384, 512), BF16),
            pltpu.VMEM((4, 384, 512), BF16),
            pltpu.VMEM((4, 192, 512), BF16),
            pltpu.VMEM((4, 192, 512), BF16),
            pltpu.VMEM((4, 384, 512), BF16),
            pltpu.VMEM((4, 384, 512), BF16),
            pltpu.VMEM((384, 512), F32),
            pltpu.VMEM((512, 1536), BF16),
            pltpu.VMEM((4, 12, 128, 1024), BF16),
            pltpu.VMEM((4, 8, 512, 128), BF16),
            pltpu.VMEM((4, 2, 256, 128), BF16),
            pltpu.VMEM((4, 2, 3, 512, 128), BF16),
            pltpu.VMEM((8, 8, 128), F32),
            pltpu.VMEM((8, 8, 128), F32),
            pltpu.VMEM((4, 8, 128), F32),
            pltpu.SemaphoreType.DMA((N_SEMS,)),
            pltpu.SemaphoreType.DMA((N_SEMS,)),
            pltpu.SemaphoreType.DMA((H + 1,)),
        ],
        compiler_params=pltpu.CompilerParams(
            collective_id=0, has_side_effects=True, vmem_limit_bytes=64_000_000
        ),
        name="lanczos",
    )(mpo, rows, left_env.reshape(12, 128, 1024), right_env.reshape(12, 128, 1024))
    return out.reshape(1, 4, 4, 128, 128), coef[0, :2]


def solution(mesh):
    torus = Mesh(
        mesh.devices.reshape(4, 2, mesh.shape["rb"], mesh.shape["wa"]), ("lb_0", "lb_1", "rb", "wa")
    )
    in_specs = (
        P("wa", None, None, LB, "rb"),
        P(None, None, LB, "wa", None),
        P(None, None, "rb", "wa", None),
        P(),
        P(),
    )
    out_specs = (P("wa", None, None, LB, "rb"), P())
    return jax.shard_map(body, mesh=torus, in_specs=in_specs, out_specs=out_specs, check_vma=False)
```

time: 424 us -> 154 us (0.36); the launches traced: 417 us -> 154 us
  waiting for transfers between devices: 200 us -> 0 us
  Pallas kernels: 0 us -> 146 us
  local copies, waits for them, and re-layouts: 95.2 us -> 6.21 us
  blocking collectives: 78.3 us -> 0 us
  matrix products: 23 us -> 0 us
  between operations: 15.8 us -> 0.66 us
    pallas_call x0 -> x1, Pallas kernels: none -> 146 us  [body(): pl.pallas_call(kernel, out_shape=(jax.ShapeDtypeStruct((4, 512, 128), F32...]
    unnamed x5 -> x0, waiting for transfers between devices: 132 us -> none
    unnamed x18 -> x4, local copies, waits for them, and re-layouts: 87.8 us -> 3.17 us
    all_gather x1 -> x0, waiting for transfers between devices: 68.3 us -> none  [piecewise(): outs.append(jax.vmap(apply)(lax.all_gather(piece, axis), starts))]
    all_to_all x2 -> x0, blocking collectives: 42.5 us -> none  [the longest x1 30 us: sent_to_all(): return lax.all_to_all(copies, axis, split_axis=0, concat_axis=0, tiled=True)]
    psum x4 -> x0, blocking collectives: 35.7 us -> none  [over_axes(): return functools.reduce(lax.psum, axes, x)]
    dot_general x4 -> x0, matrix products: 23 us -> none  [the longest x1 10.6 us: right_term(): jnp.einsum('pcvhtn,vhndq->cdtpq', shard_piece, right_env, preferred_eleme...]
    another operation x2 -> x0, local copies, waits for them, and re-layouts: 5.45 us -> none
  transfers between devices with their start and end apart: 3 -> 0, of which waited for: 3 -> 0; matrix products, arithmetic and copies ran while one was open for 0% -> 0% of each run, Pallas kernels for 0% -> 0%
where the time goes in v1:
time: 154 us
  Pallas kernels  146 us (95%)
  local copies, waits for them, and re-layouts  6.21 us (4%)
    pallas_call x1, Pallas kernels, body(): pl.pallas_call(kernel, out_shape=(jax.ShapeDtypeStruct((4, 512, 128), F32...  146 us
    unnamed x4, local copies, waits for them, and re-layouts  3.17 us

profile of v1, /device:TPU:1, one launch (start us, length us, event | category | flops | bytes accessed | tf_op | source)
XLA Modules:
  0.0 153.7 jit_solution(448901063989160442)
XLA Ops:
  0.6 0.0 copy-start
  0.6 0.9 copy.13
  1.5 0.8 multiply_reduce_fusion
  2.3 0.3 copy.14
  2.6 0.7 reshape.24.mpo
  3.3 0.0 copy-done
  3.3 0.9 copy_bitcast_fusion.state
  4.2 146.0 %lanczos.1 = (f32[4,512,128]{2,1,0:T(8,128)}, f32[8,128]{1,0:T(8,128)}) custom-call(f32[144]{0:T(256)} %reshape.24.mpo, bf16[4,128,512]{2,1,0:T(8,128)(2,1)} %copy_bitcast_fusion.state, bf16[12,128,1024]{2,1,0:T(8,128)(2,1)} %bitcast.13, bf16[12,128,1024]{2,1,0:T(8,128)(2,1)} %bitcast.14), custom_call_target="tpu_custom_call" | custom-call | tf_op jit(solution)/shard_map/lanczos/pallas_call | solution.py:473
  150.2 1.2 slice_bitcast_fusion
  151.4 2.3 %copy.19 = f32[1,4,4,128,128]{4,3,2,1,0:T(8,128)} copy(f32[1,4,4,128,128]{4,3,2,1,0:T(8,128)} %bitcast.15) | data formatting | bytes 2097152
Async XLA Ops:
  0.6 2.7 %copy-start = (bf16[1,4,4,128,128]{4,3,2,1,0:T(8,128)(2,1)S(1)}, bf16[1,4,4,128,128]{4,3,2,1,0:T(8,128)(2,1)}, u32[]{:S(2)}) copy-start(bf16[1,4,4,128,128]{4,3,2,1,0:T(8,128)(2,1)} %param.5) | copy-start | bytes 1572868

commit v2 on v1

v2 whole, which is shorter than its diff:
```python
import functools

import jax
import jax.numpy as jnp
from jax import lax
from jax.experimental import pallas as pl
from jax.experimental.pallas import tpu as pltpu
from jax.sharding import Mesh
from jax.sharding import PartitionSpec as P

LB = ("lb_0", "lb_1")
EPSILON = 1e-06
ENTRIES = 4.0 * 4 * 4 * 1024 * 1024
F32, BF16 = jnp.float32, jnp.bfloat16
X, Y, Z, H = 4, 4, 8, 4
N_SEMS = 240
ITEMS = 8
UNITS = tuple((m, i) for m in range(2) for i in (0, 1, 3, 2))


ORDER = (
    "own.0", "turn.0", "near.0", "own.1", "turn.1", "rest.0", "own.2", "turn.2",
    "blocks.0", "left.0", "direct.0",
    "near.1", "rest.1", "own.3", "near.2", "rest.2", "blocks.1", "left.1", "far.0", "direct.1",
    "near.3", "rest.3", "envs", "blocks.2", "left.2", "far.1", "direct.2",
    "mix.0", "blocks.3", "left.3", "far.2", "direct.3",
    "left.4", "mix.1", "penvs.0", "far.3", "direct.4",
    "left.5", "mix.2", "far.4", "direct.5",
    "penvs.1", "left.6", "mix.3", "con.0", "far.5", "direct.6", "hop.0.2",
    "left.7", "hop.0.3", "mix.4", "hop.0.4", "far.6", "direct.7",
    "penvs.2", "mix.5", "con.1", "con.2", "far.7", "hop.1.2", "hop.2.2", "mix.6", "hop.1.3", "hop.2.3",
    "mix.7", "con.4", "hop.1.4", "hop.2.4", "con.5", "con.6", "hop.4.2", "hop.5.2", "hop.6.2", "fenvs",
    "hop.4.3", "hop.5.3", "con.3", "con.7", "hop.6.3", "hop.4.4", "hop.3.2", "hop.5.4", "hop.7.2", "hop.6.4",
    "fin.0", "fin.1", "fin.2", "hop.3.3", "hop.7.3", "fin.4", "fin.5", "fin.6",
    "hop.3.4", "hop.7.4", "fin.3", "fin.7",
)


def staged(f):
    def run(*args):
        with jax.named_scope(f"{f.__name__}#" + "_".join(str(a) for a in args if isinstance(a, int))):
            return f(*args)

    return run


def matmul(a, b):
    return lax.dot_general(a, b, (((1,), (0,)), ((), ())), preferred_element_type=F32)


def step(
    one,
    two,
    state_in,
    left_in,
    right_in,
    out,
    coef,
    state,
    left,
    pair,
    blocks,
    left_other,
    left_t,
    far,
    up,
    down,
    up_own,
    down_own,
    here,
    up_far,
    down_far,
    from_below,
    from_above,
    mixed,
    envs,
    image,
    ring_half,
    ring_full,
    sums_z,
    sums_xy,
    send_sems,
    recv_sems,
    local_sems,
):
    y, c, z, x = (lax.axis_index(a) for a in ("lb_0", "lb_1", "rb", "wa"))
    other = 1 - c

    def at(dx=0, dy=0, dz=0, core=None):
        return (
            lax.rem(y + dy, Y),
            c if core is None else core,
            lax.rem(z + dz, Z),
            lax.rem(x + dx, X),
        )

    used = []

    def copy(src, dst, device):
        k = len(used)
        used.append(
            pltpu.make_async_remote_copy(
                src_ref=src,
                dst_ref=dst,
                send_sem=send_sems.at[k],
                recv_sem=recv_sems.at[k],
                device_id=device,
                device_id_type=pl.DeviceIdType.MESH,
            )
        )
        return used[-1]

    partner = at(core=other)
    x_up, x_down = at(dx=1), at(dx=X - 1)
    y_up, y_down = at(dy=1), at(dy=Y - 1)
    z_up, z_down = at(dz=1), at(dz=Z - 1)
    z_peers = [at(dz=k) for k in range(1, Z)]
    xy_peers = [
        at(dx=i, dy=j, core=core)
        for i in range(X)
        for j in range(Y)
        for core in (c, other)
        if not (i == 0 and j == 0 and core is c)
    ]

    barrier = pltpu.get_barrier_semaphore()
    peers = z_peers + xy_peers
    for peer in peers:
        pl.semaphore_signal(barrier, inc=1, device_id=peer, device_id_type=pl.DeviceIdType.MESH)

    own = x * 2 + c
    load_state = pltpu.make_async_copy(state_in, state, local_sems.at[H + 1])
    load_left = pltpu.make_async_copy(left_in, left, local_sems.at[H + 2])
    local = [
        pltpu.make_async_copy(state_in.at[pl.ds(h * 4, 4)], blocks.at[h, own], local_sems.at[h])
        for h in range(H)
    ]
    local.append(pltpu.make_async_copy(right_in, envs.at[0], local_sems.at[H]))
    for item in [load_state, load_left] + local:
        item.start()

    with jax.named_scope("pairs"):
        for w in range(3):
            for v in range(3):
                for s in range(4):
                    for t in range(4):
                        total = sum(
                            one[w, s // 2, t // 2, u] * two[u, s % 2, t % 2, v] for u in range(3)
                        )
                        k = ((w * 3 + v) * 4 + s) * 4 + t
                        pair[k] = jnp.full((8, 128), total, F32)
    with jax.named_scope("entry"):
        load_state.wait()
        pl.semaphore_wait(barrier, len(peers))

    g_below = lax.rem(x + X - 1, X) * 2 + c
    g_above = lax.rem(x + 1, X) * 2 + c
    g_far = lax.rem(x + 2, X) * 2 + c
    lo, hi = pl.ds(0, 2), pl.ds(2, 2)
    mine = [state.at[pl.ds(h * 4, 4)] for h in range(H)]

    def send_mine(h, parts, device):
        return [copy(mine[h].at[part], blocks.at[h, own, part], device) for part in parts]

    whole = (pl.ds(0, 4),)
    b_up = [send_mine(h, (lo, hi) if h == 0 else whole, x_up) for h in range(H)]
    b_down = [send_mine(h, (hi, lo) if h == 0 else whole, x_down) for h in range(H)]
    b_own = [copy(mine[h], blocks.at[h, own], partner) for h in range(H)]
    bf_up = [copy(blocks.at[h, g_below, lo], blocks.at[h, g_below, lo], x_up) for h in range(H)]
    bf_down = [copy(blocks.at[h, g_above, hi], blocks.at[h, g_above, hi], x_down) for h in range(H)]
    b_pass = [
        [
            copy(blocks.at[h, g_below], blocks.at[h, g_below], partner),
            copy(blocks.at[h, g_above], blocks.at[h, g_above], partner),
            copy(blocks.at[h, g_far, lo], blocks.at[h, g_far, lo], partner),
            copy(blocks.at[h, g_far, hi], blocks.at[h, g_far, hi], partner),
        ]
        for h in range(H)
    ]

    @staged
    def start_own(h):
        for pair_of in zip(b_up[h], b_down[h]):
            for item in pair_of:
                item.start()
        b_own[h].start()

    @staged
    def pass_near(h):
        b_up[h][0].wait_recv()
        bf_up[h].start()
        b_down[h][0].wait_recv()
        bf_down[h].start()

    @staged
    def pass_rest(h):
        for item in b_up[h][1:]:
            item.wait_recv()
        b_pass[h][0].start()
        for item in b_down[h][1:]:
            item.wait_recv()
        b_pass[h][1].start()

    @staged
    def get_blocks(h):
        bf_up[h].wait_recv()
        b_pass[h][2].start()
        bf_down[h].wait_recv()
        b_pass[h][3].start()
        local[h].wait()
        b_own[h].wait_recv()
        for item in b_pass[h]:
            item.wait_recv()

    a_swap = [
        copy(
            left.at[:, :, pl.ds(pl.multiple_of(k * 256 + other * 128, 128), 128)],
            left_other.at[k],
            partner,
        )
        for k in range(Y)
    ]

    def put_left(r, w, g, core, tile):
        cols = pl.ds(pl.multiple_of((g * 2 + core) * 128, 128), 128)
        rows = pl.ds(pl.multiple_of(r * 192 + w * 64, 64), 64)
        turned = tile.T
        left_t[0, rows, cols] = turned[:64]
        left_t[1, rows, cols] = turned[64:]

    def transpose_own(i, _):
        for r in range(Y):
            cols = pl.ds(pl.multiple_of(lax.rem(y + r, Y) * 256 + c * 128, 128), 128)
            put_left(r, i // 4, lax.rem(i, 4), c, left[i, :, cols])
        return 0

    def transpose_other(i, _):
        for r in range(Y):
            put_left(r, i // 4, lax.rem(i, 4), other, left_other[lax.rem(y + r, Y), i])
        return 0

    top, low = pl.ds(0, 96), pl.ds(96, 96)
    items = range(ITEMS)
    c_far_up = [copy(far.at[i, top], up_far.at[i], y_up) for i in items]
    c_far_down = [copy(far.at[i, low], down_far.at[i], y_down) for i in items]
    c_up_low = [copy(up.at[i, low], from_below.at[i, low], y_up) for i in items]
    c_down_top = [copy(down.at[i, top], from_above.at[i, top], y_down) for i in items]
    c_up_top = [copy(up.at[i, top], from_below.at[i, top], y_up) for i in items]
    c_down_low = [copy(down.at[i, low], from_above.at[i, low], y_down) for i in items]

    @staged
    def left_item(i):
        m, h = divmod(i, H)

        def tile(j, _):
            cols = pl.ds(pl.multiple_of(j * 256, 256), 256)
            b = jnp.concatenate(
                [blocks[h, :, j * 2].reshape(1024, 128), blocks[h, :, j * 2 + 1].reshape(1024, 128)],
                axis=1,
            )
            value = matmul(left_t[m], b)
            far[i, :, cols] = value[384:576].astype(BF16)
            up_own[i, :, cols] = value[192:288]
            up[i, low, cols] = value[288:384].astype(BF16)
            down[i, top, cols] = value[576:672].astype(BF16)
            down_own[i, :, cols] = value[672:768]
            here[i, :, cols] = value[:192]
            return 0

        lax.fori_loop(0, 2, tile, 0)
        c_far_up[i].start()
        c_far_down[i].start()

    @staged
    def start_direct(i):
        c_up_low[i].start()
        c_down_top[i].start()

    @staged
    def pass_far(i):
        c_far_up[i].wait_recv()
        up[i, top] = (up_own[i] + up_far[i].astype(F32)).astype(BF16)
        c_up_top[i].start()
        c_far_down[i].wait_recv()
        down[i, low] = (down_own[i] + down_far[i].astype(F32)).astype(BF16)
        c_down_low[i].start()

    @staged
    def mix(i):
        m, h = divmod(i, H)
        for item in (c_up_low[i], c_down_top[i], c_up_top[i], c_down_low[i]):
            item.wait_recv()

        def rows_of(k, _):
            start = pl.multiple_of(k * 16, 16)
            parts = []
            for w in range(3):
                for s in range(4):
                    at_ws = (i, pl.ds(w * 64 + start, 16), slice(s * 128, (s + 1) * 128))
                    part = here[at_ws] + from_below[at_ws].astype(F32) + from_above[at_ws].astype(F32)
                    parts.append(part.reshape(2, 8, 128))
            for v in range(3):
                for t in range(4):
                    total = None
                    for w in range(3):
                        for s in range(4):
                            term = pair[((w * 3 + v) * 4 + s) * 4 + t][None] * parts[w * 4 + s]
                            total = term if total is None else total + term
                    k = v * 4 + h
                    mixed[m, pl.ds(t * 64 + start, 16), k * 128 : (k + 1) * 128] = total.reshape(
                        16, 128
                    ).astype(BF16)
            return 0

        lax.fori_loop(0, 4, rows_of, 0)

    pieces = [pl.ds(c * 6 + 2 * k, 2) for k in range(3)]
    q_lo, q_hi = pl.ds(c * 6, 3), pl.ds(c * 6 + 3, 3)
    r_up = [copy(envs.at[0, p], envs.at[3, p], x_up) for p in pieces]
    r_down = [copy(envs.at[0, p], envs.at[1, p], x_down) for p in pieces]
    rp_below = [copy(envs.at[3, p], envs.at[3, p], partner) for p in pieces]
    rp_above = [copy(envs.at[1, p], envs.at[1, p], partner) for p in pieces]
    rf_up = copy(envs.at[3, q_lo], envs.at[2, q_lo], x_up)
    rf_down = copy(envs.at[1, q_hi], envs.at[2, q_hi], x_down)
    rp_lo = copy(envs.at[2, q_lo], envs.at[2, q_lo], partner)
    rp_hi = copy(envs.at[2, q_hi], envs.at[2, q_hi], partner)

    @staged
    def start_envs():
        local[H].wait()
        for k in range(3):
            r_up[k].start()
            r_down[k].start()

    @staged
    def pass_envs(k):
        r_up[k].wait_recv()
        rp_below[k].start()
        r_down[k].wait_recv()
        rp_above[k].start()
        if k == 2:
            rf_up.start()
            rf_down.start()

    @staged
    def pass_far_envs():
        rf_up.wait_recv()
        rp_lo.start()
        rf_down.wait_recv()
        rp_hi.start()

    def zmod(k):
        return lax.rem(z + k, Z)

    first, second = pl.ds(0, 128), pl.ds(128, 128)
    rings = []
    for u in range(8):
        ring = {}
        ring[1] = (
            copy(image.at[u, zmod(4), first], ring_half.at[u, 0], z_up),
            copy(image.at[u, zmod(4), second], ring_half.at[u, 1], z_down),
        )
        for k in (2, 3, 4):
            ring[k] = (
                copy(image.at[u, zmod(5 - k)], ring_full.at[u, 0, k - 2], z_up),
                copy(image.at[u, zmod(3 + k)], ring_full.at[u, 1, k - 2], z_down),
            )
        rings.append(ring)

    waited = set()

    @staged
    def contract(u):
        m, i = UNITS[u]
        for item in {0: [], 1: rp_above, 3: rp_below, 2: [rp_lo, rp_hi]}[i]:
            if id(item) not in waited:
                waited.add(id(item))
                item.wait_recv()

        def tile(j, _):
            cols = pl.ds(pl.multiple_of(j * 256, 256), 256)
            value = matmul(mixed[m], envs[i, :, :, cols].reshape(1536, 256)).astype(BF16)
            image[u, j * 2] = value[:, :128]
            image[u, j * 2 + 1] = value[:, 128:]
            return 0

        lax.fori_loop(0, 4, tile, 0)
        hop(u, 1)

    def add_into(u, k, rows, term):
        image[u, k, rows] = (image[u, k, rows].astype(F32) + term.astype(F32)).astype(BF16)

    @staged
    def hop(u, k):
        for side in range(2):
            if k > 1:
                rings[u][k - 1][side].wait_recv()
                owner = zmod(5 - k) if side == 0 else zmod(3 + k)
                if k == 2:
                    add_into(u, owner, (first, second)[side], ring_half[u, side])
                else:
                    add_into(u, owner, pl.ds(0, 256), ring_full[u, side, k - 3])
            rings[u][k][side].start()

    zero = jnp.zeros((8, 128), F32)

    def folded(value):
        return jnp.sum(value.reshape(-1, 8, 128), axis=0)

    @staged
    def finish(u, sums):
        rings[u][4][0].wait_recv()
        rings[u][4][1].wait_recv()
        m, i = UNITS[u]
        h = lax.rem(x + i, X)

        def piece(s, sums):
            squares, crossed, images = sums
            rows = pl.ds(pl.multiple_of(s * 64, 64), 64)
            value = (
                image[u, z, rows].astype(F32)
                + ring_full[u, 0, 2, rows].astype(F32)
                + ring_full[u, 1, 2, rows].astype(F32)
            )
            out[h * 4 + s, pl.ds(m * 64, 64)] = value
            start = state[h * 4 + s, pl.ds(m * 64, 64)].astype(F32)
            return (
                squares + folded(start * start),
                crossed + folded(start * value),
                images + folded(value * value),
            )

        return lax.fori_loop(0, 4, piece, sums)

    @staged
    def turn(k):
        if k == 0:
            load_left.wait()
            for item in a_swap:
                item.start()
            lax.fori_loop(0, 12, transpose_own, 0)
        if k == 1:
            for item in a_swap:
                item.wait_recv()
        if k == 2:
            lax.fori_loop(0, 12, transpose_other, 0)

    state_sums = (zero, zero, zero)
    stages = {
        "own": start_own,
        "near": pass_near,
        "rest": pass_rest,
        "turn": turn,
        "blocks": get_blocks,
        "left": left_item,
        "direct": start_direct,
        "far": pass_far,
        "mix": mix,
        "envs": start_envs,
        "penvs": pass_envs,
        "fenvs": pass_far_envs,
        "con": contract,
        "hop": hop,
    }
    for line in ORDER:
        name, *numbers = line.split(".")
        numbers = [int(n) for n in numbers]
        if name == "fin":
            state_sums = finish(numbers[0], state_sums)
        else:
            stages[name](*numbers)

    @staged
    def all_sum(phase, values, slots, me, targets):
        slots[me] = values
        sends = [copy(slots.at[me], slots.at[me], target) for target in targets]
        for item in sends:
            item.start()
        for item in sends:
            item.wait_recv()
        return jnp.sum(slots[...], axis=0)

    lane = lax.broadcasted_iota(jnp.int32, (1, 128), 1)
    packed = jnp.zeros((1, 128), F32)
    for k, value in enumerate(state_sums):
        packed = jnp.where(lane == k, jnp.sum(value, keepdims=True), packed)
    packed = all_sum(0, packed, sums_z, z, z_peers)
    packed = all_sum(1, packed, sums_xy, (x * Y + y) * 2 + c, xy_peers)
    square, projection, image_square = (
        jnp.sum(jnp.where(lane == k, packed, 0.0), keepdims=True) * (1.0 / ENTRIES) for k in range(3)
    )
    norm_sq = square + EPSILON
    alpha = projection / norm_sq
    residual_sq = (image_square - 2.0 * alpha * projection + alpha * alpha * square) / norm_sq
    beta = jnp.sqrt(residual_sq + EPSILON)
    scale = 1.0 / (jnp.sqrt(norm_sq) * beta)
    coef[0] = alpha[0, 0]
    coef[1] = beta[0, 0]

    def scaled(i, _):
        out[i] = (out[i] - alpha * state[i].astype(F32)) * scale
        return 0

    with jax.named_scope("scaled"):
        lax.fori_loop(0, 16, scaled, 0)
    with jax.named_scope("drain"):
        for item in used:
            item.wait_send()


def kernel(*refs):
    pl.run_scoped(
        functools.partial(step, *refs),
        pltpu.SemaphoreType.DMA((N_SEMS,)),
        pltpu.SemaphoreType.DMA((N_SEMS,)),
        pltpu.SemaphoreType.DMA((H + 3,)),
    )


def body(state, left_env, right_env, site_one, site_two):
    vmem = pl.BlockSpec(memory_space=pltpu.VMEM)
    smem = pl.BlockSpec(memory_space=pltpu.SMEM)
    anywhere = pl.BlockSpec(memory_space=pl.ANY)
    out, coef = pl.pallas_call(
        kernel,
        out_shape=(
            jax.ShapeDtypeStruct((16, 128, 128), F32),
            jax.ShapeDtypeStruct((2,), F32),
        ),
        in_specs=[smem, smem, anywhere, anywhere, anywhere],
        out_specs=(vmem, smem),
        scratch_shapes=[
            pltpu.VMEM((16, 128, 128), BF16),
            pltpu.VMEM((12, 128, 1024), BF16),
            pltpu.VMEM((144, 8, 128), F32),
            pltpu.VMEM((4, 8, 4, 128, 128), BF16),
            pltpu.VMEM((4, 12, 128, 128), BF16),
            pltpu.VMEM((2, 768, 1024), BF16),
            pltpu.VMEM((ITEMS, 192, 512), BF16),
            pltpu.VMEM((ITEMS, 192, 512), BF16),
            pltpu.VMEM((ITEMS, 192, 512), BF16),
            pltpu.VMEM((ITEMS, 96, 512), F32),
            pltpu.VMEM((ITEMS, 96, 512), F32),
            pltpu.VMEM((ITEMS, 192, 512), F32),
            pltpu.VMEM((ITEMS, 96, 512), BF16),
            pltpu.VMEM((ITEMS, 96, 512), BF16),
            pltpu.VMEM((ITEMS, 192, 512), BF16),
            pltpu.VMEM((ITEMS, 192, 512), BF16),
            pltpu.VMEM((2, 256, 1536), BF16),
            pltpu.VMEM((4, 12, 128, 1024), BF16),
            pltpu.VMEM((8, 8, 256, 128), BF16),
            pltpu.VMEM((8, 2, 128, 128), BF16),
            pltpu.VMEM((8, 2, 3, 256, 128), BF16),
            pltpu.VMEM((8, 1, 128), F32),
            pltpu.VMEM((32, 1, 128), F32),
        ],
        compiler_params=pltpu.CompilerParams(
            collective_id=0, has_side_effects=True, vmem_limit_bytes=64_000_000
        ),
        name="lanczos",
    )(
        site_one.transpose(0, 2, 3, 1),
        site_two.transpose(0, 2, 3, 1),
        state.reshape(16, 128, 128),
        left_env.reshape(12, 128, 1024),
        right_env.reshape(12, 128, 1024),
    )
    return out.reshape(1, 4, 4, 128, 128), coef


def solution(mesh):
    torus = Mesh(
        mesh.devices.reshape(4, 2, mesh.shape["rb"], mesh.shape["wa"]), ("lb_0", "lb_1", "rb", "wa")
    )
    in_specs = (
        P("wa", None, None, LB, "rb"),
        P(None, None, LB, "wa", None),
        P(None, None, "rb", "wa", None),
        P(),
        P(),
    )
    out_specs = (P("wa", None, None, LB, "rb"), P())
    return jax.shard_map(body, mesh=torus, in_specs=in_specs, out_specs=out_specs, check_vma=False)
```

time: 154 us -> 132 us (0.86)
  Pallas kernels: 146 us -> 127 us
  local copies, waits for them, and re-layouts: 6.21 us -> 3.41 us
    pallas_call x1, Pallas kernels: 146 us -> 127 us  [body(): pl.pallas_call(kernel, out_shape=(jax.ShapeDtypeStruct((16, 128, 128), F3...]
    reshape x2 -> x0, local copies, waits for them, and re-layouts: 1.59 us -> none  [the longest x1 0.85 us: body(): state.reshape(4, 4, 128, 128).transpose(0, 2, 1, 3).reshape(4, 128, 512)]
    unnamed x4 -> x2, local copies, waits for them, and re-layouts: 3.17 us -> 3.41 us
where the time goes in v2:
time: 132 us; the launch traced here: 131 us
  Pallas kernels  127 us (96%)
  local copies, waits for them, and re-layouts  3.41 us (3%)
    pallas_call x1, Pallas kernels, body(): pl.pallas_call(kernel, out_shape=(jax.ShapeDtypeStruct((16, 128, 128), F3...  127 us
    unnamed x2, local copies, waits for them, and re-layouts  3.41 us

profile of v2, /device:TPU:1, one launch (start us, length us, event | category | flops | bytes accessed | tf_op | source)
XLA Modules:
  0.0 131.5 jit_solution(11823522201977574092)
XLA Ops:
  0.6 127.4 %lanczos.1 = (f32[16,128,128]{2,1,0:T(8,128)}, f32[2]{0:T(128)}) custom-call(f32[3,2,2,3]{3,2,1,0:T(2,128)} %bitcast.10, f32[3,2,2,3]{3,2,1,0:T(2,128)} %bitcast.11, bf16[16,128,128]{2,1,0:T(8,128)(2,1)} %bitcast.9, bf16[12,128,1024]{2,1,0:T(8,128)(2,1)} %bitcast.6, bf16[12,128,1024]{2,1,0:T(8,128)(2,1)} %bitcast.7), custom_call_target="tpu_custom_call" | custom-call | tf_op jit(solution)/shard_map/lanczos/pallas_call | solution.py:524
  128.1 2.3 %copy.9 = f32[1,4,4,128,128]{4,3,2,1,0:T(8,128)} copy(f32[1,4,4,128,128]{4,3,2,1,0:T(8,128)} %bitcast.8) | data formatting | bytes 2097152
  130.4 1.1 copy.10

commit v3 on v2

--- a/solution.py
+++ b/solution.py
@@ -19,20 +19,16 @@
 
 
 ORDER = (
-    "own.0", "turn.0", "near.0", "own.1", "turn.1", "rest.0", "own.2", "turn.2",
-    "blocks.0", "left.0", "direct.0",
-    "near.1", "rest.1", "own.3", "near.2", "rest.2", "blocks.1", "left.1", "far.0", "direct.1",
-    "near.3", "rest.3", "envs", "blocks.2", "left.2", "far.1", "direct.2",
-    "mix.0", "blocks.3", "left.3", "far.2", "direct.3",
-    "left.4", "mix.1", "penvs.0", "far.3", "direct.4",
-    "left.5", "mix.2", "far.4", "direct.5",
-    "penvs.1", "left.6", "mix.3", "con.0", "far.5", "direct.6", "hop.0.2",
-    "left.7", "hop.0.3", "mix.4", "hop.0.4", "far.6", "direct.7",
-    "penvs.2", "mix.5", "con.1", "con.2", "far.7", "hop.1.2", "hop.2.2", "mix.6", "hop.1.3", "hop.2.3",
-    "mix.7", "con.4", "hop.1.4", "hop.2.4", "con.5", "con.6", "hop.4.2", "hop.5.2", "hop.6.2", "fenvs",
-    "hop.4.3", "hop.5.3", "con.3", "con.7", "hop.6.3", "hop.4.4", "hop.3.2", "hop.5.4", "hop.7.2", "hop.6.4",
-    "fin.0", "fin.1", "fin.2", "hop.3.3", "hop.7.3", "fin.4", "fin.5", "fin.6",
-    "hop.3.4", "hop.7.4", "fin.3", "fin.7",
+    "own.1", "own.0", "near.1", "turn.3", "own.2", "turn.0", "near.0", "own.3", "rest.1", "turn.1", "turn.2",
+    "rest.0", "blocks.1", "left.5", "near.2", "left.1", "near.3", "direct.1", "envs.0", "blocks.0", "rest.3",
+    "left.4", "rest.2", "blocks.2", "far.1", "left.2", "envs.1", "blocks.3", "left.3", "left.0", "direct.0",
+    "far.3", "far.0", "penvs.0", "far.2", "direct.3", "direct.2", "far.4", "mix.1", "envs.2", "left.7",
+    "direct.4", "mix.3", "left.6", "mix.0", "mix.2", "far.5", "direct.7", "penvs.1", "con.0", "penvs.2",
+    "hop.0.2", "mix.4", "far.7", "direct.5", "con.1", "far.6", "direct.6", "hop.0.3", "con.2", "hop.1.2",
+    "mix.7", "hop.2.2", "mix.5", "hop.0.4", "hop.1.3", "mix.6", "con.4", "hop.2.3", "con.5", "hop.1.4",
+    "con.6", "hop.4.2", "hop.2.4", "fenvs", "hop.5.2", "hop.6.2", "con.3", "hop.4.3", "con.7", "fin.0",
+    "hop.5.3", "hop.3.2", "fin.2", "hop.7.2", "hop.6.3", "hop.5.4", "hop.3.3", "hop.7.3", "hop.6.4",
+    "hop.4.4", "fin.5", "hop.3.4", "fin.1", "hop.7.4", "fin.6", "fin.4", "fin.3", "fin.7",
 )
 
 
@@ -49,13 +45,16 @@
 
 
 def step(
-    one,
-    two,
+    one_in,
+    two_in,
     state_in,
     left_in,
     right_in,
     out,
     coef,
+    applied,
+    one,
+    two,
     state,
     left,
     pair,
@@ -124,22 +123,26 @@
     ]
 
     barrier = pltpu.get_barrier_semaphore()
-    peers = z_peers + xy_peers
+    peers = [partner, x_up, x_down, y_up, y_down, z_up, z_down]
     for peer in peers:
         pl.semaphore_signal(barrier, inc=1, device_id=peer, device_id_type=pl.DeviceIdType.MESH)
 
     own = x * 2 + c
     load_state = pltpu.make_async_copy(state_in, state, local_sems.at[H + 1])
     load_left = pltpu.make_async_copy(left_in, left, local_sems.at[H + 2])
+    load_sites = [
+        pltpu.make_async_copy(one_in, one, local_sems.at[H + 3]),
+        pltpu.make_async_copy(two_in, two, local_sems.at[H + 4]),
+    ]
     local = [
         pltpu.make_async_copy(state_in.at[pl.ds(h * 4, 4)], blocks.at[h, own], local_sems.at[h])
         for h in range(H)
     ]
     local.append(pltpu.make_async_copy(right_in, envs.at[0], local_sems.at[H]))
-    for item in [load_state, load_left] + local:
+    for item in load_sites + [load_state, load_left] + local:
         item.start()
 
-    with jax.named_scope("pairs"):
+    def fill_pairs():
         for w in range(3):
             for v in range(3):
                 for s in range(4):
@@ -149,6 +152,7 @@
                         )
                         k = ((w * 3 + v) * 4 + s) * 4 + t
                         pair[k] = jnp.full((8, 128), total, F32)
+
     with jax.named_scope("entry"):
         load_state.wait()
         pl.semaphore_wait(barrier, len(peers))
@@ -162,9 +166,8 @@
     def send_mine(h, parts, device):
         return [copy(mine[h].at[part], blocks.at[h, own, part], device) for part in parts]
 
-    whole = (pl.ds(0, 4),)
-    b_up = [send_mine(h, (lo, hi) if h == 0 else whole, x_up) for h in range(H)]
-    b_down = [send_mine(h, (hi, lo) if h == 0 else whole, x_down) for h in range(H)]
+    b_up = [send_mine(h, (lo, hi), x_up) for h in range(H)]
+    b_down = [send_mine(h, (hi, lo), x_down) for h in range(H)]
     b_own = [copy(mine[h], blocks.at[h, own], partner) for h in range(H)]
     bf_up = [copy(blocks.at[h, g_below, lo], blocks.at[h, g_below, lo], x_up) for h in range(H)]
     bf_down = [copy(blocks.at[h, g_above, hi], blocks.at[h, g_above, hi], x_down) for h in range(H)]
@@ -326,11 +329,11 @@
     rp_hi = copy(envs.at[2, q_hi], envs.at[2, q_hi], partner)
 
     @staged
-    def start_envs():
-        local[H].wait()
-        for k in range(3):
-            r_up[k].start()
-            r_down[k].start()
+    def start_envs(k):
+        if k == 0:
+            local[H].wait()
+        r_up[k].start()
+        r_down[k].start()
 
     @staged
     def pass_envs(k):
@@ -422,7 +425,7 @@
                 + ring_full[u, 0, 2, rows].astype(F32)
                 + ring_full[u, 1, 2, rows].astype(F32)
             )
-            out[h * 4 + s, pl.ds(m * 64, 64)] = value
+            applied[h * 4 + s, pl.ds(m * 64, 64)] = value
             start = state[h * 4 + s, pl.ds(m * 64, 64)].astype(F32)
             return (
                 squares + folded(start * start),
@@ -430,7 +433,11 @@
                 images + folded(value * value),
             )
 
-        return lax.fori_loop(0, 4, piece, sums)
+        sums = lax.fori_loop(0, 4, piece, sums)
+        done = (pl.ds(h * 4, 4), pl.ds(m * 64, 64))
+        local.append(pltpu.make_async_copy(applied.at[done], out.at[done], local_sems.at[H + 5 + u]))
+        local[-1].start()
+        return sums
 
     @staged
     def turn(k):
@@ -444,6 +451,10 @@
                 item.wait_recv()
         if k == 2:
             lax.fori_loop(0, 12, transpose_other, 0)
+        if k == 3:
+            for item in load_sites:
+                item.wait()
+            fill_pairs()
 
     state_sums = (zero, zero, zero)
     stages = {
@@ -494,18 +505,13 @@
     residual_sq = (image_square - 2.0 * alpha * projection + alpha * alpha * square) / norm_sq
     beta = jnp.sqrt(residual_sq + EPSILON)
     scale = 1.0 / (jnp.sqrt(norm_sq) * beta)
-    coef[0] = alpha[0, 0]
-    coef[1] = beta[0, 0]
-
-    def scaled(i, _):
-        out[i] = (out[i] - alpha * state[i].astype(F32)) * scale
-        return 0
-
-    with jax.named_scope("scaled"):
-        lax.fori_loop(0, 16, scaled, 0)
+    for k, value in enumerate((alpha, beta, scale)):
+        coef[k] = value[0, 0]
     with jax.named_scope("drain"):
         for item in used:
             item.wait_send()
+        for item in local[H + 1 :]:
+            item.wait()
 
 
 def kernel(*refs):
@@ -513,23 +519,55 @@
         functools.partial(step, *refs),
         pltpu.SemaphoreType.DMA((N_SEMS,)),
         pltpu.SemaphoreType.DMA((N_SEMS,)),
-        pltpu.SemaphoreType.DMA((H + 3,)),
+        pltpu.SemaphoreType.DMA((H + 13,)),
     )
 
 
+def normalize(applied_in, state_in, terms_in, out, coef, applied, state, result, terms, sems):
+    load_terms = pltpu.make_async_copy(terms_in, terms, sems.at[0])
+    load_terms.start()
+    parts = [pl.ds(4 * k, 4) for k in range(4)]
+    loads, stores = [], []
+    for k, part in enumerate(parts):
+        loads.append(pltpu.make_async_copy(applied_in.at[part], applied.at[part], sems.at[1 + k]))
+        loads.append(pltpu.make_async_copy(state_in.at[part], state.at[part], sems.at[5 + k]))
+        stores.append(pltpu.make_async_copy(result.at[part], out.at[part], sems.at[9 + k]))
+    for item in loads:
+        item.start()
+    load_terms.wait()
+    alpha, beta, scale = (terms[k] for k in range(3))
+    coef[0] = alpha
+    coef[1] = beta
+    for k in range(4):
+        loads[2 * k].wait()
+        loads[2 * k + 1].wait()
+
+        def rows_of(i, _):
+            result[i] = (applied[i] - alpha * state[i].astype(F32)) * scale
+            return 0
+
+        lax.fori_loop(4 * k, 4 * k + 4, rows_of, 0)
+        stores[k].start()
+    for item in stores:
+        item.wait()
+
+
 def body(state, left_env, right_env, site_one, site_two):
-    vmem = pl.BlockSpec(memory_space=pltpu.VMEM)
     smem = pl.BlockSpec(memory_space=pltpu.SMEM)
     anywhere = pl.BlockSpec(memory_space=pl.ANY)
-    out, coef = pl.pallas_call(
+    state = state.reshape(16, 128, 128)
+    applied, terms = pl.pallas_call(
         kernel,
         out_shape=(
             jax.ShapeDtypeStruct((16, 128, 128), F32),
-            jax.ShapeDtypeStruct((2,), F32),
+            jax.ShapeDtypeStruct((3,), F32),
         ),
-        in_specs=[smem, smem, anywhere, anywhere, anywhere],
-        out_specs=(vmem, smem),
+        in_specs=[anywhere] * 5,
+        out_specs=(anywhere, smem),
         scratch_shapes=[
+            pltpu.VMEM((16, 128, 128), F32),
+            pltpu.SMEM((3, 2, 2, 3), F32),
+            pltpu.SMEM((3, 2, 2, 3), F32),
             pltpu.VMEM((16, 128, 128), BF16),
             pltpu.VMEM((12, 128, 1024), BF16),
             pltpu.VMEM((144, 8, 128), F32),
@@ -561,10 +599,28 @@
     )(
         site_one.transpose(0, 2, 3, 1),
         site_two.transpose(0, 2, 3, 1),
-        state.reshape(16, 128, 128),
+        state,
         left_env.reshape(12, 128, 1024),
         right_env.reshape(12, 128, 1024),
     )
+    out, coef = pl.pallas_call(
+        normalize,
+        out_shape=(
+            jax.ShapeDtypeStruct((16, 128, 128), F32),
+            jax.ShapeDtypeStruct((2,), F32),
+        ),
+        in_specs=[anywhere] * 3,
+        out_specs=(anywhere, smem),
+        scratch_shapes=[
+            pltpu.VMEM((16, 128, 128), F32),
+            pltpu.VMEM((16, 128, 128), BF16),
+            pltpu.VMEM((16, 128, 128), F32),
+            pltpu.SMEM((3,), F32),
+            pltpu.SemaphoreType.DMA((13,)),
+        ],
+        compiler_params=pltpu.CompilerParams(vmem_limit_bytes=64_000_000),
+        name="normalize",
+    )(applied, state, terms)
     return out.reshape(1, 4, 4, 128, 128), coef
 
 

time: 132 us -> 121 us (0.917)
  Pallas kernels: 127 us -> 121 us
  local copies, waits for them, and re-layouts: 3.41 us -> 0 us
    pallas_call x1, Pallas kernels: 127 us -> 118 us  [body(): pl.pallas_call(kernel, out_shape=(jax.ShapeDtypeStruct((16, 128, 128), F3...]
    unnamed x2 -> x0, local copies, waits for them, and re-layouts: 3.41 us -> none
    pallas_call x0 -> x1, Pallas kernels: none -> 2.74 us  [body(): pl.pallas_call(normalize, out_shape=(jax.ShapeDtypeStruct((16, 128, 128),...]
where the time goes in v3:
time: 121 us
  Pallas kernels  121 us (100%)
    pallas_call x1, Pallas kernels, body(): pl.pallas_call(kernel, out_shape=(jax.ShapeDtypeStruct((16, 128, 128), F3...  118 us
    pallas_call x1, Pallas kernels, body(): pl.pallas_call(normalize, out_shape=(jax.ShapeDtypeStruct((16, 128, 128),...  2.74 us

profile of v3, /device:TPU:1, one launch (start us, length us, event | category | flops | bytes accessed | tf_op | source)
XLA Modules:
  0.0 121.3 jit_solution(16735284839420252995)
XLA Ops:
  0.6 117.9 %lanczos.1 = (f32[16,128,128]{2,1,0:T(8,128)}, f32[3]{0:T(128)}) custom-call(f32[3,2,2,3]{3,2,1,0:T(2,128)} %bitcast.10, f32[3,2,2,3]{3,2,1,0:T(2,128)} %bitcast.11, bf16[16,128,128]{2,1,0:T(8,128)(2,1)} %bitcast.8, bf16[12,128,1024]{2,1,0:T(8,128)(2,1)} %bitcast.6, bf16[12,128,1024]{2,1,0:T(8,128)(2,1)} %bitcast.7), custom_call_target="tpu_custom_call" | custom-call | tf_op jit(solution)/shard_map/lanczos/pallas_call | solution.py:559
  118.6 2.7 %normalize.1 = (f32[16,128,128]{2,1,0:T(8,128)}, f32[2]{0:T(128)}) custom-call(f32[16,128,128]{2,1,0:T(8,128)} %get-tuple-element.6.applied_in, bf16[16,128,128]{2,1,0:T(8,128)(2,1)} %bitcast.9, f32[3]{0:T(128)} %get-tuple-element.7.terms_in), custom_call_target="tpu_custom_call" | custom-call | tf_op jit(solution)/shard_map/normalize/pallas_call | solution.py:606

commit v4 on v3

--- a/solution.py
+++ b/solution.py
@@ -13,22 +13,27 @@
 ENTRIES = 4.0 * 4 * 4 * 1024 * 1024
 F32, BF16 = jnp.float32, jnp.bfloat16
 X, Y, Z, H = 4, 4, 8, 4
-N_SEMS = 240
+N_SEMS = 300
 ITEMS = 8
-UNITS = tuple((m, i) for m in range(2) for i in (0, 1, 3, 2))
+UNITS = tuple((m, i, p) for m in range(2) for i in (0, 1, 3, 2) for p in range(2))
 
 
 ORDER = (
-    "own.1", "own.0", "near.1", "turn.3", "own.2", "turn.0", "near.0", "own.3", "rest.1", "turn.1", "turn.2",
-    "rest.0", "blocks.1", "left.5", "near.2", "left.1", "near.3", "direct.1", "envs.0", "blocks.0", "rest.3",
-    "left.4", "rest.2", "blocks.2", "far.1", "left.2", "envs.1", "blocks.3", "left.3", "left.0", "direct.0",
-    "far.3", "far.0", "penvs.0", "far.2", "direct.3", "direct.2", "far.4", "mix.1", "envs.2", "left.7",
-    "direct.4", "mix.3", "left.6", "mix.0", "mix.2", "far.5", "direct.7", "penvs.1", "con.0", "penvs.2",
-    "hop.0.2", "mix.4", "far.7", "direct.5", "con.1", "far.6", "direct.6", "hop.0.3", "con.2", "hop.1.2",
-    "mix.7", "hop.2.2", "mix.5", "hop.0.4", "hop.1.3", "mix.6", "con.4", "hop.2.3", "con.5", "hop.1.4",
-    "con.6", "hop.4.2", "hop.2.4", "fenvs", "hop.5.2", "hop.6.2", "con.3", "hop.4.3", "con.7", "fin.0",
-    "hop.5.3", "hop.3.2", "fin.2", "hop.7.2", "hop.6.3", "hop.5.4", "hop.3.3", "hop.7.3", "hop.6.4",
-    "hop.4.4", "fin.5", "hop.3.4", "fin.1", "hop.7.4", "fin.6", "fin.4", "fin.3", "fin.7",
+    "own.3", "own.0", "turn.0", "near.3", "turn.1", "turn.2", "own.1", "rest.3", "near.0", "own.2",
+    "blocks.3", "near.1", "left.7", "left.3", "rest.0", "direct.7", "envs.0", "rest.1", "blocks.0", "near.2",
+    "left.0", "envs.1", "envs.2", "blocks.1", "rest.2", "left.1", "direct.0", "far.0", "direct.1", "direct.3",
+    "blocks.2", "left.2", "envs.3", "far.1", "direct.2", "turn.3", "far.2", "mix.0", "penvs.0", "far.3",
+    "mix.1", "left.6", "left.4", "penvs.1", "left.5", "far.7", "mix.2", "penvs.2", "mix.3", "direct.4",
+    "con.1", "rf.0", "direct.5", "con.0", "con.4", "hop.0.2", "con.2", "far.5", "hop.4.2", "far.4", "hop.2.2",
+    "penvs.3", "mix.7", "hop.1.2", "hop.0.3", "hop.4.3", "hop.2.3", "direct.6", "con.3", "con.5", "hop.1.3",
+    "hop.3.2", "far.6", "rf.1", "hop.0.4", "fenvs.0", "mix.5", "hop.5.2", "hop.1.4", "hop.4.4", "mix.4",
+    "hop.2.4", "con.6", "hop.3.3", "mix.6", "con.12", "hop.5.3", "con.8", "con.14", "hop.6.2", "con.10",
+    "hop.3.4", "con.11", "fin.4", "con.9", "hop.5.4", "hop.6.3", "fenvs.1", "fin.0", "con.13", "hop.8.2",
+    "hop.11.2", "hop.12.2", "hop.9.2", "con.15", "hop.13.2", "fin.3", "con.7", "hop.14.2", "hop.8.3",
+    "hop.15.2", "hop.7.2", "fin.2", "hop.12.3", "hop.14.3", "hop.10.2", "hop.9.3", "fin.5", "fin.1",
+    "hop.11.3", "hop.6.4", "hop.13.3", "hop.15.3", "hop.7.3", "hop.14.4", "hop.10.3", "hop.11.4", "hop.9.4",
+    "hop.8.4", "hop.15.4", "hop.12.4", "hop.13.4", "hop.10.4", "fin.6", "fin.9", "hop.7.4", "fin.13",
+    "fin.15", "fin.14", "fin.11", "fin.12", "fin.8", "fin.7", "fin.10",
 )
 
 
@@ -74,8 +79,8 @@
     mixed,
     envs,
     image,
-    ring_half,
-    ring_full,
+    ring,
+    totals,
     sums_z,
     sums_xy,
     send_sems,
@@ -138,8 +143,15 @@
         pltpu.make_async_copy(state_in.at[pl.ds(h * 4, 4)], blocks.at[h, own], local_sems.at[h])
         for h in range(H)
     ]
-    local.append(pltpu.make_async_copy(right_in, envs.at[0], local_sems.at[H]))
-    for item in load_sites + [load_state, load_left] + local:
+    load_right = [
+        pltpu.make_async_copy(
+            right_in.at[:, :, pl.ds(b * 128, 128)],
+            envs.at[0, b % 2 * 4 + b // 2],
+            local_sems.at[H + 5 + b],
+        )
+        for b in range(Z)
+    ]
+    for item in load_sites + [load_state, load_left] + local + load_right:
         item.start()
 
     def fill_pairs():
@@ -317,21 +329,24 @@
 
         lax.fori_loop(0, 4, rows_of, 0)
 
-    pieces = [pl.ds(c * 6 + 2 * k, 2) for k in range(3)]
+    half = pl.ds(c * 6, 6)
     q_lo, q_hi = pl.ds(c * 6, 3), pl.ds(c * 6 + 3, 3)
-    r_up = [copy(envs.at[0, p], envs.at[3, p], x_up) for p in pieces]
-    r_down = [copy(envs.at[0, p], envs.at[1, p], x_down) for p in pieces]
-    rp_below = [copy(envs.at[3, p], envs.at[3, p], partner) for p in pieces]
-    rp_above = [copy(envs.at[1, p], envs.at[1, p], partner) for p in pieces]
-    rf_up = copy(envs.at[3, q_lo], envs.at[2, q_lo], x_up)
-    rf_down = copy(envs.at[1, q_hi], envs.at[2, q_hi], x_down)
-    rp_lo = copy(envs.at[2, q_lo], envs.at[2, q_lo], partner)
-    rp_hi = copy(envs.at[2, q_hi], envs.at[2, q_hi], partner)
+    pieces = [(pl.ds(2 * k, 2), half) for k in range(4)]
+    r_up = [copy(envs.at[0, *q], envs.at[3, *q], x_up) for q in pieces]
+    r_down = [copy(envs.at[0, *q], envs.at[1, *q], x_down) for q in pieces]
+    rp_below = [copy(envs.at[3, *q], envs.at[3, *q], partner) for q in pieces]
+    rp_above = [copy(envs.at[1, *q], envs.at[1, *q], partner) for q in pieces]
+    group = [pl.ds(4 * p, 4) for p in range(2)]
+    rf_up = [copy(envs.at[3, g, q_lo], envs.at[2, g, q_lo], x_up) for g in group]
+    rf_down = [copy(envs.at[1, g, q_hi], envs.at[2, g, q_hi], x_down) for g in group]
+    rp_lo = [copy(envs.at[2, g, q_lo], envs.at[2, g, q_lo], partner) for g in group]
+    rp_hi = [copy(envs.at[2, g, q_hi], envs.at[2, g, q_hi], partner) for g in group]
 
     @staged
     def start_envs(k):
         if k == 0:
-            local[H].wait()
+            for item in load_right:
+                item.wait()
         r_up[k].start()
         r_down[k].start()
 
@@ -341,103 +356,129 @@
         rp_below[k].start()
         r_down[k].wait_recv()
         rp_above[k].start()
-        if k == 2:
-            rf_up.start()
-            rf_down.start()
-
-    @staged
-    def pass_far_envs():
-        rf_up.wait_recv()
-        rp_lo.start()
-        rf_down.wait_recv()
-        rp_hi.start()
+
+    @staged
+    def start_far_envs(p):
+        rf_up[p].start()
+        rf_down[p].start()
+
+    @staged
+    def pass_far_envs(p):
+        rf_up[p].wait_recv()
+        rp_lo[p].start()
+        rf_down[p].wait_recv()
+        rp_hi[p].start()
 
     def zmod(k):
         return lax.rem(z + k, Z)
 
-    first, second = pl.ds(0, 128), pl.ds(128, 128)
-    rings = []
-    for u in range(8):
-        ring = {}
-        ring[1] = (
-            copy(image.at[u, zmod(4), first], ring_half.at[u, 0], z_up),
-            copy(image.at[u, zmod(4), second], ring_half.at[u, 1], z_down),
+    parity = lax.rem(z, 2)
+
+    def has_role(p, hop):
+        return parity == (p if hop % 2 == 1 else 1 - p)
+
+    first, second, every = pl.ds(0, 128), pl.ds(128, 128), pl.ds(0, 256)
+    places = {1: None, 2: 0, 3: 0, 4: 1}
+    hops = []
+    for u in range(len(UNITS)):
+        sends = {}
+        sends[1] = (
+            copy(image.at[u, zmod(4) // 2, first], ring.at[u, 0, 1, first], z_up),
+            copy(image.at[u, zmod(4) // 2, second], ring.at[u, 1, 1, first], z_down),
         )
         for k in (2, 3, 4):
-            ring[k] = (
-                copy(image.at[u, zmod(5 - k)], ring_full.at[u, 0, k - 2], z_up),
-                copy(image.at[u, zmod(3 + k)], ring_full.at[u, 1, k - 2], z_down),
+            sends[k] = (
+                copy(image.at[u, zmod(5 - k) // 2], ring.at[u, 0, places[k]], z_up),
+                copy(image.at[u, zmod(3 + k) // 2], ring.at[u, 1, places[k]], z_down),
             )
-        rings.append(ring)
+        hops.append(sends)
+    hop_copies = {id(item) for sends in hops for k in sends for item in sends[k]}
 
     waited = set()
 
     @staged
     def contract(u):
-        m, i = UNITS[u]
-        for item in {0: [], 1: rp_above, 3: rp_below, 2: [rp_lo, rp_hi]}[i]:
+        m, i, p = UNITS[u]
+        needed = {
+            0: [],
+            1: rp_above[2 * p : 2 * p + 2],
+            3: rp_below[2 * p : 2 * p + 2],
+            2: [rp_lo[p], rp_hi[p]],
+        }[i]
+        for item in needed:
             if id(item) not in waited:
                 waited.add(id(item))
                 item.wait_recv()
 
         def tile(j, _):
-            cols = pl.ds(pl.multiple_of(j * 256, 256), 256)
-            value = matmul(mixed[m], envs[i, :, :, cols].reshape(1536, 256)).astype(BF16)
+            b = jnp.concatenate(
+                [envs[i, p * 4 + j * 2 + k].reshape(1536, 128) for k in range(2)], axis=1
+            )
+            value = matmul(mixed[m], b).astype(BF16)
             image[u, j * 2] = value[:, :128]
             image[u, j * 2 + 1] = value[:, 128:]
             return 0
 
-        lax.fori_loop(0, 4, tile, 0)
-        hop(u, 1)
-
-    def add_into(u, k, rows, term):
-        image[u, k, rows] = (image[u, k, rows].astype(F32) + term.astype(F32)).astype(BF16)
+        lax.fori_loop(0, 2, tile, 0)
+
+        @pl.when(has_role(p, 1))
+        def _():
+            for item in hops[u][1]:
+                item.start()
 
     @staged
     def hop(u, k):
-        for side in range(2):
-            if k > 1:
-                rings[u][k - 1][side].wait_recv()
-                owner = zmod(5 - k) if side == 0 else zmod(3 + k)
+        @pl.when(has_role(UNITS[u][2], k))
+        def _():
+            for side in range(2):
+                hops[u][k - 1][side].wait_recv()
+                e = (zmod(5 - k) if side == 0 else zmod(3 + k)) // 2
                 if k == 2:
-                    add_into(u, owner, (first, second)[side], ring_half[u, side])
+                    rows, term = (first, second)[side], ring[u, side, 1, first]
                 else:
-                    add_into(u, owner, pl.ds(0, 256), ring_full[u, side, k - 3])
-            rings[u][k][side].start()
-
-    zero = jnp.zeros((8, 128), F32)
+                    rows, term = every, ring[u, side, places[k - 1]]
+                image[u, e, rows] = (image[u, e, rows].astype(F32) + term.astype(F32)).astype(BF16)
+                hops[u][k][side].start()
 
     def folded(value):
         return jnp.sum(value.reshape(-1, 8, 128), axis=0)
 
-    @staged
-    def finish(u, sums):
-        rings[u][4][0].wait_recv()
-        rings[u][4][1].wait_recv()
-        m, i = UNITS[u]
+    stores = []
+
+    @staged
+    def finish(u):
+        m, i, p = UNITS[u]
         h = lax.rem(x + i, X)
-
-        def piece(s, sums):
-            squares, crossed, images = sums
-            rows = pl.ds(pl.multiple_of(s * 64, 64), 64)
-            value = (
-                image[u, z, rows].astype(F32)
-                + ring_full[u, 0, 2, rows].astype(F32)
-                + ring_full[u, 1, 2, rows].astype(F32)
-            )
-            applied[h * 4 + s, pl.ds(m * 64, 64)] = value
-            start = state[h * 4 + s, pl.ds(m * 64, 64)].astype(F32)
-            return (
-                squares + folded(start * start),
-                crossed + folded(start * value),
-                images + folded(value * value),
-            )
-
-        sums = lax.fori_loop(0, 4, piece, sums)
         done = (pl.ds(h * 4, 4), pl.ds(m * 64, 64))
-        local.append(pltpu.make_async_copy(applied.at[done], out.at[done], local_sems.at[H + 5 + u]))
-        local[-1].start()
-        return sums
+        stores.append(
+            (p, pltpu.make_async_copy(applied.at[done], out.at[done], local_sems.at[H + 13 + u]))
+        )
+
+        @pl.when(has_role(p, 1))
+        def _():
+            for side in range(2):
+                hops[u][4][side].wait_recv()
+
+            def piece(s, sums):
+                squares, crossed, images = sums
+                rows = pl.ds(pl.multiple_of(s * 64, 64), 64)
+                value = (
+                    image[u, z // 2, rows].astype(F32)
+                    + ring[u, 0, 1, rows].astype(F32)
+                    + ring[u, 1, 1, rows].astype(F32)
+                )
+                applied[h * 4 + s, pl.ds(m * 64, 64)] = value
+                start = state[h * 4 + s, pl.ds(m * 64, 64)].astype(F32)
+                return (
+                    squares + folded(start * start),
+                    crossed + folded(start * value),
+                    images + folded(value * value),
+                )
+
+            sums = lax.fori_loop(0, 4, piece, (totals[0], totals[1], totals[2]))
+            for k in range(3):
+                totals[k] = sums[k]
+            stores[-1][1].start()
 
     @staged
     def turn(k):
@@ -456,7 +497,7 @@
                 item.wait()
             fill_pairs()
 
-    state_sums = (zero, zero, zero)
+    totals[...] = jnp.zeros((3, 8, 128), F32)
     stages = {
         "own": start_own,
         "near": pass_near,
@@ -469,17 +510,16 @@
         "mix": mix,
         "envs": start_envs,
         "penvs": pass_envs,
+        "rf": start_far_envs,
         "fenvs": pass_far_envs,
+        "fin": finish,
         "con": contract,
         "hop": hop,
     }
     for line in ORDER:
         name, *numbers = line.split(".")
         numbers = [int(n) for n in numbers]
-        if name == "fin":
-            state_sums = finish(numbers[0], state_sums)
-        else:
-            stages[name](*numbers)
+        stages[name](*numbers)
 
     @staged
     def all_sum(phase, values, slots, me, targets):
@@ -493,8 +533,8 @@
 
     lane = lax.broadcasted_iota(jnp.int32, (1, 128), 1)
     packed = jnp.zeros((1, 128), F32)
-    for k, value in enumerate(state_sums):
-        packed = jnp.where(lane == k, jnp.sum(value, keepdims=True), packed)
+    for k in range(3):
+        packed = jnp.where(lane == k, jnp.sum(totals[k], keepdims=True), packed)
     packed = all_sum(0, packed, sums_z, z, z_peers)
     packed = all_sum(1, packed, sums_xy, (x * Y + y) * 2 + c, xy_peers)
     square, projection, image_square = (
@@ -509,9 +549,19 @@
         coef[k] = value[0, 0]
     with jax.named_scope("drain"):
         for item in used:
-            item.wait_send()
-        for item in local[H + 1 :]:
-            item.wait()
+            if id(item) not in hop_copies:
+                item.wait_send()
+        for p in range(2):
+
+            @pl.when(has_role(p, 1))
+            def _():
+                for (_, _, q), sends in zip(UNITS, hops):
+                    for k in (1, 3) if q == p else (2, 4):
+                        for item in sends[k]:
+                            item.wait_send()
+                for q, item in stores:
+                    if q == p:
+                        item.wait()
 
 
 def kernel(*refs):
@@ -519,7 +569,7 @@
         functools.partial(step, *refs),
         pltpu.SemaphoreType.DMA((N_SEMS,)),
         pltpu.SemaphoreType.DMA((N_SEMS,)),
-        pltpu.SemaphoreType.DMA((H + 13,)),
+        pltpu.SemaphoreType.DMA((H + 29,)),
     )
 
 
@@ -585,10 +635,10 @@
             pltpu.VMEM((ITEMS, 192, 512), BF16),
             pltpu.VMEM((ITEMS, 192, 512), BF16),
             pltpu.VMEM((2, 256, 1536), BF16),
-            pltpu.VMEM((4, 12, 128, 1024), BF16),
-            pltpu.VMEM((8, 8, 256, 128), BF16),
-            pltpu.VMEM((8, 2, 128, 128), BF16),
-            pltpu.VMEM((8, 2, 3, 256, 128), BF16),
+            pltpu.VMEM((4, 8, 12, 128, 128), BF16),
+            pltpu.VMEM((16, 4, 256, 128), BF16),
+            pltpu.VMEM((16, 2, 2, 256, 128), BF16),
+            pltpu.VMEM((3, 8, 128), F32),
             pltpu.VMEM((8, 1, 128), F32),
             pltpu.VMEM((32, 1, 128), F32),
         ],

time: 121 us -> 119 us (0.983)
  Pallas kernels: 121 us -> 118 us
    pallas_call x1, Pallas kernels: 118 us -> 115 us  [body(): pl.pallas_call(kernel, out_shape=(jax.ShapeDtypeStruct((16, 128, 128), F3...]
where the time goes in v4:
time: 119 us
  Pallas kernels  118 us (99%)
    pallas_call x1, Pallas kernels, body(): pl.pallas_call(kernel, out_shape=(jax.ShapeDtypeStruct((16, 128, 128), F3...  115 us
    pallas_call x1, Pallas kernels, body(): pl.pallas_call(normalize, out_shape=(jax.ShapeDtypeStruct((16, 128, 128),...  2.74 us

profile of v4, /device:TPU:1, one launch (start us, length us, event | category | flops | bytes accessed | tf_op | source)
XLA Modules:
  0.0 118.6 jit_solution(8899823334785661942)
XLA Ops:
  0.6 115.3 %lanczos.1 = (f32[16,128,128]{2,1,0:T(8,128)}, f32[3]{0:T(128)}) custom-call(f32[3,2,2,3]{3,2,1,0:T(2,128)} %bitcast.10, f32[3,2,2,3]{3,2,1,0:T(2,128)} %bitcast.11, bf16[16,128,128]{2,1,0:T(8,128)(2,1)} %bitcast.8, bf16[12,128,1024]{2,1,0:T(8,128)(2,1)} %bitcast.6, bf16[12,128,1024]{2,1,0:T(8,128)(2,1)} %bitcast.7), custom_call_target="tpu_custom_call" | custom-call | tf_op jit(solution)/shard_map/lanczos/pallas_call | solution.py:609
  115.9 2.7 %normalize.1 = (f32[16,128,128]{2,1,0:T(8,128)}, f32[2]{0:T(128)}) custom-call(f32[16,128,128]{2,1,0:T(8,128)} %get-tuple-element.6.applied_in, bf16[16,128,128]{2,1,0:T(8,128)(2,1)} %bitcast.9, f32[3]{0:T(128)} %get-tuple-element.7.terms_in), custom_call_target="tpu_custom_call" | custom-call | tf_op jit(solution)/shard_map/normalize/pallas_call | solution.py:656

commit v5 on v4

--- a/solution.py
+++ b/solution.py
@@ -13,27 +13,42 @@
 ENTRIES = 4.0 * 4 * 4 * 1024 * 1024
 F32, BF16 = jnp.float32, jnp.bfloat16
 X, Y, Z, H = 4, 4, 8, 4
-N_SEMS = 300
-ITEMS = 8
-UNITS = tuple((m, i, p) for m in range(2) for i in (0, 1, 3, 2) for p in range(2))
-
-
+N_SEMS = 440
+ROWS = (64, 32, 32)
+STARTS = tuple(sum(ROWS[:m]) for m in range(len(ROWS)))
+TOPS = tuple((3 * r // 16 + (m + 1) % 2) // 2 * 16 for m, r in enumerate(ROWS))
+TOP_STARTS = tuple(sum(TOPS[:m]) for m in range(len(ROWS)))
+TOP_ROWS = sum(TOPS)
+ITEMS = 4 * len(ROWS)
+UNITS = tuple((m, i, p) for m in range(len(ROWS)) for i in (0, 1, 3, 2) for p in range(2))
+
+
+OWN, TURN, NEAR, REST, BLOCKS, LEFT, DIRECT, FAR, MIX, ENVS, PENVS, RF, FENVS, CON, HOP, FIN = range(16)
 ORDER = (
-    "own.3", "own.0", "turn.0", "near.3", "turn.1", "turn.2", "own.1", "rest.3", "near.0", "own.2",
-    "blocks.3", "near.1", "left.7", "left.3", "rest.0", "direct.7", "envs.0", "rest.1", "blocks.0", "near.2",
-    "left.0", "envs.1", "envs.2", "blocks.1", "rest.2", "left.1", "direct.0", "far.0", "direct.1", "direct.3",
-    "blocks.2", "left.2", "envs.3", "far.1", "direct.2", "turn.3", "far.2", "mix.0", "penvs.0", "far.3",
-    "mix.1", "left.6", "left.4", "penvs.1", "left.5", "far.7", "mix.2", "penvs.2", "mix.3", "direct.4",
-    "con.1", "rf.0", "direct.5", "con.0", "con.4", "hop.0.2", "con.2", "far.5", "hop.4.2", "far.4", "hop.2.2",
-    "penvs.3", "mix.7", "hop.1.2", "hop.0.3", "hop.4.3", "hop.2.3", "direct.6", "con.3", "con.5", "hop.1.3",
-    "hop.3.2", "far.6", "rf.1", "hop.0.4", "fenvs.0", "mix.5", "hop.5.2", "hop.1.4", "hop.4.4", "mix.4",
-    "hop.2.4", "con.6", "hop.3.3", "mix.6", "con.12", "hop.5.3", "con.8", "con.14", "hop.6.2", "con.10",
-    "hop.3.4", "con.11", "fin.4", "con.9", "hop.5.4", "hop.6.3", "fenvs.1", "fin.0", "con.13", "hop.8.2",
-    "hop.11.2", "hop.12.2", "hop.9.2", "con.15", "hop.13.2", "fin.3", "con.7", "hop.14.2", "hop.8.3",
-    "hop.15.2", "hop.7.2", "fin.2", "hop.12.3", "hop.14.3", "hop.10.2", "hop.9.3", "fin.5", "fin.1",
-    "hop.11.3", "hop.6.4", "hop.13.3", "hop.15.3", "hop.7.3", "hop.14.4", "hop.10.3", "hop.11.4", "hop.9.4",
-    "hop.8.4", "hop.15.4", "hop.12.4", "hop.13.4", "hop.10.4", "fin.6", "fin.9", "hop.7.4", "fin.13",
-    "fin.15", "fin.14", "fin.11", "fin.12", "fin.8", "fin.7", "fin.10",
+    (OWN, 1), (TURN, 0), (OWN, 3), (NEAR, 1), (TURN, 1), (OWN, 0), (TURN, 2), (REST, 1), (TURN, 3), (OWN, 2),
+    (NEAR, 3), (BLOCKS, 1), (LEFT, 1), (LEFT, 9), (DIRECT, 1), (NEAR, 0), (REST, 3), (NEAR, 2), (REST, 2),
+    (ENVS, 0), (ENVS, 1), (FAR, 1), (REST, 0), (ENVS, 2), (BLOCKS, 3), (DIRECT, 9), (LEFT, 3), (DIRECT, 3),
+    (BLOCKS, 2), (LEFT, 2), (DIRECT, 2), (BLOCKS, 0), (LEFT, 0), (DIRECT, 0), (PENVS, 0), (FAR, 2), (FAR, 3),
+    (MIX, 1), (FAR, 0), (ENVS, 3), (PENVS, 1), (LEFT, 8), (RF, 0), (LEFT, 11), (MIX, 2), (LEFT, 10),
+    (DIRECT, 8), (MIX, 3), (MIX, 0), (FAR, 9), (CON, 0), (FAR, 8), (CON, 1), (DIRECT, 11), (CON, 2), (CON, 4),
+    (FAR, 11), (HOP, 0, 2), (DIRECT, 10), (HOP, 1, 2), (FAR, 10), (MIX, 9), (LEFT, 6), (LEFT, 7), (MIX, 8),
+    (LEFT, 5), (HOP, 4, 2), (PENVS, 2), (DIRECT, 6), (LEFT, 4), (MIX, 11), (HOP, 2, 2), (PENVS, 3),
+    (HOP, 1, 3), (HOP, 0, 3), (MIX, 10), (CON, 16), (DIRECT, 5), (CON, 20), (CON, 18), (HOP, 4, 3), (FAR, 6),
+    (RF, 1), (CON, 17), (CON, 5), (HOP, 2, 3), (CON, 19), (CON, 21), (HOP, 16, 2), (FAR, 5), (HOP, 1, 4),
+    (DIRECT, 4), (CON, 3), (HOP, 18, 2), (HOP, 20, 2), (FAR, 4), (FAR, 7), (HOP, 2, 4), (HOP, 17, 2),
+    (HOP, 5, 2), (HOP, 19, 2), (HOP, 0, 4), (HOP, 21, 2), (DIRECT, 7), (FENVS, 0), (HOP, 3, 2), (MIX, 5),
+    (HOP, 4, 4), (MIX, 6), (CON, 22), (MIX, 4), (HOP, 20, 3), (HOP, 17, 3), (CON, 6), (HOP, 5, 3),
+    (HOP, 16, 3), (MIX, 7), (CON, 8), (CON, 13), (CON, 12), (HOP, 21, 3), (HOP, 19, 3), (CON, 10),
+    (HOP, 18, 3), (HOP, 17, 4), (CON, 9), (CON, 14), (HOP, 3, 3), (HOP, 5, 4), (FENVS, 1), (HOP, 13, 2),
+    (HOP, 21, 4), (CON, 11), (HOP, 9, 2), (HOP, 3, 4), (HOP, 22, 2), (HOP, 8, 2), (HOP, 12, 2), (FIN, 1),
+    (CON, 7), (HOP, 11, 2), (CON, 23), (HOP, 10, 2), (HOP, 20, 4), (HOP, 22, 3), (HOP, 7, 2), (HOP, 23, 2),
+    (CON, 15), (HOP, 14, 2), (HOP, 12, 3), (HOP, 6, 2), (HOP, 16, 4), (HOP, 13, 3), (FIN, 4), (HOP, 15, 2),
+    (HOP, 10, 3), (HOP, 14, 3), (HOP, 6, 3), (FIN, 16), (HOP, 9, 3), (HOP, 18, 4), (HOP, 13, 4), (FIN, 2),
+    (FIN, 17), (HOP, 11, 3), (FIN, 0), (HOP, 23, 3), (HOP, 9, 4), (HOP, 7, 3), (HOP, 8, 3), (HOP, 15, 3),
+    (HOP, 11, 4), (HOP, 12, 4), (HOP, 23, 4), (FIN, 20), (FIN, 5), (FIN, 18), (HOP, 7, 4), (HOP, 15, 4),
+    (HOP, 22, 4), (HOP, 10, 4), (HOP, 14, 4), (HOP, 6, 4), (HOP, 8, 4), (FIN, 11), (HOP, 19, 4), (FIN, 22),
+    (FIN, 14), (FIN, 21), (FIN, 12), (FIN, 10), (FIN, 9), (FIN, 3), (FIN, 6), (FIN, 23), (FIN, 7), (FIN, 8),
+    (FIN, 19), (FIN, 13), (FIN, 15),
 )
 
 
@@ -238,10 +253,10 @@
 
     def put_left(r, w, g, core, tile):
         cols = pl.ds(pl.multiple_of((g * 2 + core) * 128, 128), 128)
-        rows = pl.ds(pl.multiple_of(r * 192 + w * 64, 64), 64)
         turned = tile.T
-        left_t[0, rows, cols] = turned[:64]
-        left_t[1, rows, cols] = turned[64:]
+        for start, count in zip(STARTS, ROWS):
+            row = pl.multiple_of(12 * start + 3 * r * count + w * count, 16)
+            left_t[pl.ds(row, count), cols] = turned[start : start + count]
 
     def transpose_own(i, _):
         for r in range(Y):
@@ -254,18 +269,28 @@
             put_left(r, i // 4, lax.rem(i, 4), other, left_other[lax.rem(y + r, Y), i])
         return 0
 
-    top, low = pl.ds(0, 96), pl.ds(96, 96)
-    items = range(ITEMS)
-    c_far_up = [copy(far.at[i, top], up_far.at[i], y_up) for i in items]
-    c_far_down = [copy(far.at[i, low], down_far.at[i], y_down) for i in items]
-    c_up_low = [copy(up.at[i, low], from_below.at[i, low], y_up) for i in items]
-    c_down_top = [copy(down.at[i, top], from_above.at[i, top], y_down) for i in items]
-    c_up_top = [copy(up.at[i, top], from_below.at[i, top], y_up) for i in items]
-    c_down_low = [copy(down.at[i, low], from_above.at[i, low], y_down) for i in items]
+    items = [divmod(i, H) for i in range(ITEMS)]
+    full = [pl.ds(3 * start, 3 * count) for start, count in zip(STARTS, ROWS)]
+    top = [pl.ds(3 * start, size) for start, size in zip(STARTS, TOPS)]
+    low = [
+        pl.ds(3 * start + size, 3 * count - size) for start, size, count in zip(STARTS, TOPS, ROWS)
+    ]
+    top_own = [pl.ds(start, size) for start, size in zip(TOP_STARTS, TOPS)]
+    low_own = [
+        pl.ds(3 * start - before, 3 * count - size)
+        for start, before, size, count in zip(STARTS, TOP_STARTS, TOPS, ROWS)
+    ]
+    c_far_up = [copy(far.at[h, top[m]], up_far.at[h, top_own[m]], y_up) for m, h in items]
+    c_far_down = [copy(far.at[h, low[m]], down_far.at[h, low_own[m]], y_down) for m, h in items]
+    c_up_low = [copy(up.at[h, low[m]], from_below.at[h, low[m]], y_up) for m, h in items]
+    c_down_top = [copy(down.at[h, top[m]], from_above.at[h, top[m]], y_down) for m, h in items]
+    c_up_top = [copy(up.at[h, top[m]], from_below.at[h, top[m]], y_up) for m, h in items]
+    c_down_low = [copy(down.at[h, low[m]], from_above.at[h, low[m]], y_down) for m, h in items]
 
     @staged
     def left_item(i):
-        m, h = divmod(i, H)
+        m, h = items[i]
+        n, size = 3 * ROWS[m], TOPS[m]
 
         def tile(j, _):
             cols = pl.ds(pl.multiple_of(j * 256, 256), 256)
@@ -273,13 +298,13 @@
                 [blocks[h, :, j * 2].reshape(1024, 128), blocks[h, :, j * 2 + 1].reshape(1024, 128)],
                 axis=1,
             )
-            value = matmul(left_t[m], b)
-            far[i, :, cols] = value[384:576].astype(BF16)
-            up_own[i, :, cols] = value[192:288]
-            up[i, low, cols] = value[288:384].astype(BF16)
-            down[i, top, cols] = value[576:672].astype(BF16)
-            down_own[i, :, cols] = value[672:768]
-            here[i, :, cols] = value[:192]
+            value = matmul(left_t[pl.ds(12 * STARTS[m], 4 * n)], b)
+            here[h, full[m], cols] = value[:n]
+            up_own[h, top_own[m], cols] = value[n : n + size]
+            up[h, low[m], cols] = value[n + size : 2 * n].astype(BF16)
+            far[h, full[m], cols] = value[2 * n : 3 * n].astype(BF16)
+            down[h, top[m], cols] = value[3 * n : 3 * n + size].astype(BF16)
+            down_own[h, low_own[m], cols] = value[3 * n + size :]
             return 0
 
         lax.fori_loop(0, 2, tile, 0)
@@ -293,16 +318,18 @@
 
     @staged
     def pass_far(i):
+        m, h = items[i]
+        mine_up, mine_down = (h, top_own[m]), (h, low_own[m])
         c_far_up[i].wait_recv()
-        up[i, top] = (up_own[i] + up_far[i].astype(F32)).astype(BF16)
+        up[h, top[m]] = (up_own[mine_up] + up_far[mine_up].astype(F32)).astype(BF16)
         c_up_top[i].start()
         c_far_down[i].wait_recv()
-        down[i, low] = (down_own[i] + down_far[i].astype(F32)).astype(BF16)
+        down[h, low[m]] = (down_own[mine_down] + down_far[mine_down].astype(F32)).astype(BF16)
         c_down_low[i].start()
 
     @staged
     def mix(i):
-        m, h = divmod(i, H)
+        m, h = items[i]
         for item in (c_up_low[i], c_down_top[i], c_up_top[i], c_down_low[i]):
             item.wait_recv()
 
@@ -311,7 +338,8 @@
             parts = []
             for w in range(3):
                 for s in range(4):
-                    at_ws = (i, pl.ds(w * 64 + start, 16), slice(s * 128, (s + 1) * 128))
+                    row = 3 * STARTS[m] + w * ROWS[m] + start
+                    at_ws = (h, pl.ds(row, 16), slice(s * 128, (s + 1) * 128))
                     part = here[at_ws] + from_below[at_ws].astype(F32) + from_above[at_ws].astype(F32)
                     parts.append(part.reshape(2, 8, 128))
             for v in range(3):
@@ -322,12 +350,11 @@
                             term = pair[((w * 3 + v) * 4 + s) * 4 + t][None] * parts[w * 4 + s]
                             total = term if total is None else total + term
                     k = v * 4 + h
-                    mixed[m, pl.ds(t * 64 + start, 16), k * 128 : (k + 1) * 128] = total.reshape(
-                        16, 128
-                    ).astype(BF16)
+                    row = 4 * STARTS[m] + t * ROWS[m] + start
+                    mixed[pl.ds(row, 16), k * 128 : (k + 1) * 128] = total.reshape(16, 128).astype(BF16)
             return 0
 
-        lax.fori_loop(0, 4, rows_of, 0)
+        lax.fori_loop(0, ROWS[m] // 16, rows_of, 0)
 
     half = pl.ds(c * 6, 6)
     q_lo, q_hi = pl.ds(c * 6, 3), pl.ds(c * 6 + 3, 3)
@@ -377,19 +404,26 @@
     def has_role(p, hop):
         return parity == (p if hop % 2 == 1 else 1 - p)
 
-    first, second, every = pl.ds(0, 128), pl.ds(128, 128), pl.ds(0, 256)
+    first = [pl.ds(4 * start, 2 * count) for start, count in zip(STARTS, ROWS)]
+    second = [pl.ds(4 * start + 2 * count, 2 * count) for start, count in zip(STARTS, ROWS)]
+    every = [pl.ds(4 * start, 4 * count) for start, count in zip(STARTS, ROWS)]
     places = {1: None, 2: 0, 3: 0, 4: 1}
     hops = []
     for u in range(len(UNITS)):
+        m, v = UNITS[u][0], u % 8
         sends = {}
         sends[1] = (
-            copy(image.at[u, zmod(4) // 2, first], ring.at[u, 0, 1, first], z_up),
-            copy(image.at[u, zmod(4) // 2, second], ring.at[u, 1, 1, first], z_down),
+            copy(image.at[v, zmod(4) // 2, first[m]], ring.at[v, 0, 1, first[m]], z_up),
+            copy(image.at[v, zmod(4) // 2, second[m]], ring.at[v, 1, 1, first[m]], z_down),
         )
         for k in (2, 3, 4):
-            sends[k] = (
-                copy(image.at[u, zmod(5 - k) // 2], ring.at[u, 0, places[k]], z_up),
-                copy(image.at[u, zmod(3 + k) // 2], ring.at[u, 1, places[k]], z_down),
+            sends[k] = tuple(
+                copy(
+                    image.at[v, zmod(owner) // 2, every[m]],
+                    ring.at[v, side, places[k], every[m]],
+                    device,
+                )
+                for side, owner, device in ((0, 5 - k, z_up), (1, 3 + k, z_down))
             )
         hops.append(sends)
     hop_copies = {id(item) for sends in hops for k in sends for item in sends[k]}
@@ -414,9 +448,9 @@
             b = jnp.concatenate(
                 [envs[i, p * 4 + j * 2 + k].reshape(1536, 128) for k in range(2)], axis=1
             )
-            value = matmul(mixed[m], b).astype(BF16)
-            image[u, j * 2] = value[:, :128]
-            image[u, j * 2 + 1] = value[:, 128:]
+            value = matmul(mixed[every[m]], b).astype(BF16)
+            image[u % 8, j * 2, every[m]] = value[:, :128]
+            image[u % 8, j * 2 + 1, every[m]] = value[:, 128:]
             return 0
 
         lax.fori_loop(0, 2, tile, 0)
@@ -428,16 +462,18 @@
 
     @staged
     def hop(u, k):
+        m, v = UNITS[u][0], u % 8
+
         @pl.when(has_role(UNITS[u][2], k))
         def _():
             for side in range(2):
                 hops[u][k - 1][side].wait_recv()
                 e = (zmod(5 - k) if side == 0 else zmod(3 + k)) // 2
                 if k == 2:
-                    rows, term = (first, second)[side], ring[u, side, 1, first]
+                    rows, term = (first, second)[side][m], ring[v, side, 1, first[m]]
                 else:
-                    rows, term = every, ring[u, side, places[k - 1]]
-                image[u, e, rows] = (image[u, e, rows].astype(F32) + term.astype(F32)).astype(BF16)
+                    rows, term = every[m], ring[v, side, places[k - 1], every[m]]
+                image[v, e, rows] = (image[v, e, rows].astype(F32) + term.astype(F32)).astype(BF16)
                 hops[u][k][side].start()
 
     def folded(value):
@@ -449,7 +485,8 @@
     def finish(u):
         m, i, p = UNITS[u]
         h = lax.rem(x + i, X)
-        done = (pl.ds(h * 4, 4), pl.ds(m * 64, 64))
+        v, count, rows_here = u % 8, ROWS[m], pl.ds(STARTS[m], ROWS[m])
+        done = (pl.ds(h * 4, 4), rows_here)
         stores.append(
             (p, pltpu.make_async_copy(applied.at[done], out.at[done], local_sems.at[H + 13 + u]))
         )
@@ -461,14 +498,14 @@
 
             def piece(s, sums):
                 squares, crossed, images = sums
-                rows = pl.ds(pl.multiple_of(s * 64, 64), 64)
+                rows = pl.ds(pl.multiple_of(4 * STARTS[m] + s * count, 16), count)
                 value = (
-                    image[u, z // 2, rows].astype(F32)
-                    + ring[u, 0, 1, rows].astype(F32)
-                    + ring[u, 1, 1, rows].astype(F32)
+                    image[v, z // 2, rows].astype(F32)
+                    + ring[v, 0, 1, rows].astype(F32)
+                    + ring[v, 1, 1, rows].astype(F32)
                 )
-                applied[h * 4 + s, pl.ds(m * 64, 64)] = value
-                start = state[h * 4 + s, pl.ds(m * 64, 64)].astype(F32)
+                applied[h * 4 + s, rows_here] = value
+                start = state[h * 4 + s, rows_here].astype(F32)
                 return (
                     squares + folded(start * start),
                     crossed + folded(start * value),
@@ -499,26 +536,24 @@
 
     totals[...] = jnp.zeros((3, 8, 128), F32)
     stages = {
-        "own": start_own,
-        "near": pass_near,
-        "rest": pass_rest,
-        "turn": turn,
-        "blocks": get_blocks,
-        "left": left_item,
-        "direct": start_direct,
-        "far": pass_far,
-        "mix": mix,
-        "envs": start_envs,
-        "penvs": pass_envs,
-        "rf": start_far_envs,
-        "fenvs": pass_far_envs,
-        "fin": finish,
-        "con": contract,
-        "hop": hop,
+        OWN: start_own,
+        TURN: turn,
+        NEAR: pass_near,
+        REST: pass_rest,
+        BLOCKS: get_blocks,
+        LEFT: left_item,
+        DIRECT: start_direct,
+        FAR: pass_far,
+        MIX: mix,
+        ENVS: start_envs,
+        PENVS: pass_envs,
+        RF: start_far_envs,
+        FENVS: pass_far_envs,
+        CON: contract,
+        HOP: hop,
+        FIN: finish,
     }
-    for line in ORDER:
-        name, *numbers = line.split(".")
-        numbers = [int(n) for n in numbers]
+    for name, *numbers in ORDER:
         stages[name](*numbers)
 
     @staged
@@ -569,7 +604,7 @@
         functools.partial(step, *refs),
         pltpu.SemaphoreType.DMA((N_SEMS,)),
         pltpu.SemaphoreType.DMA((N_SEMS,)),
-        pltpu.SemaphoreType.DMA((H + 29,)),
+        pltpu.SemaphoreType.DMA((H + 13 + len(UNITS),)),
     )
 
 
@@ -623,21 +658,21 @@
             pltpu.VMEM((144, 8, 128), F32),
             pltpu.VMEM((4, 8, 4, 128, 128), BF16),
             pltpu.VMEM((4, 12, 128, 128), BF16),
-            pltpu.VMEM((2, 768, 1024), BF16),
-            pltpu.VMEM((ITEMS, 192, 512), BF16),
-            pltpu.VMEM((ITEMS, 192, 512), BF16),
-            pltpu.VMEM((ITEMS, 192, 512), BF16),
-            pltpu.VMEM((ITEMS, 96, 512), F32),
-            pltpu.VMEM((ITEMS, 96, 512), F32),
-            pltpu.VMEM((ITEMS, 192, 512), F32),
-            pltpu.VMEM((ITEMS, 96, 512), BF16),
-            pltpu.VMEM((ITEMS, 96, 512), BF16),
-            pltpu.VMEM((ITEMS, 192, 512), BF16),
-            pltpu.VMEM((ITEMS, 192, 512), BF16),
-            pltpu.VMEM((2, 256, 1536), BF16),
+            pltpu.VMEM((1536, 1024), BF16),
+            pltpu.VMEM((H, 384, 512), BF16),
+            pltpu.VMEM((H, 384, 512), BF16),
+            pltpu.VMEM((H, 384, 512), BF16),
+            pltpu.VMEM((H, TOP_ROWS, 512), F32),
+            pltpu.VMEM((H, 384 - TOP_ROWS, 512), F32),
+            pltpu.VMEM((H, 384, 512), F32),
+            pltpu.VMEM((H, TOP_ROWS, 512), BF16),
+            pltpu.VMEM((H, 384 - TOP_ROWS, 512), BF16),
+            pltpu.VMEM((H, 384, 512), BF16),
+            pltpu.VMEM((H, 384, 512), BF16),
+            pltpu.VMEM((512, 1536), BF16),
             pltpu.VMEM((4, 8, 12, 128, 128), BF16),
-            pltpu.VMEM((16, 4, 256, 128), BF16),
-            pltpu.VMEM((16, 2, 2, 256, 128), BF16),
+            pltpu.VMEM((8, 4, 512, 128), BF16),
+            pltpu.VMEM((8, 2, 2, 512, 128), BF16),
             pltpu.VMEM((3, 8, 128), F32),
             pltpu.VMEM((8, 1, 128), F32),
             pltpu.VMEM((32, 1, 128), F32),

time: 119 us -> 116 us (0.975)
  Pallas kernels: 118 us -> 115 us
    pallas_call x1, Pallas kernels: 115 us -> 112 us  [body(): pl.pallas_call(kernel, out_shape=(jax.ShapeDtypeStruct((16, 128, 128), F3...]
where the time goes in v5:
time: 116 us; the launch traced here: 115 us
  Pallas kernels  115 us (99%)
    pallas_call x1, Pallas kernels, body(): pl.pallas_call(kernel, out_shape=(jax.ShapeDtypeStruct((16, 128, 128), F3...  112 us
    pallas_call x1, Pallas kernels, body(): pl.pallas_call(normalize, out_shape=(jax.ShapeDtypeStruct((16, 128, 128),...  2.74 us

profile of v5, /device:TPU:1, one launch (start us, length us, event | category | flops | bytes accessed | tf_op | source)
XLA Modules:
  0.0 115.4 jit_solution(6041897850230561529)
XLA Ops:
  0.6 111.9 %lanczos.1 = (f32[16,128,128]{2,1,0:T(8,128)}, f32[3]{0:T(128)}) custom-call(f32[3,2,2,3]{3,2,1,0:T(2,128)} %bitcast.10, f32[3,2,2,3]{3,2,1,0:T(2,128)} %bitcast.11, bf16[16,128,128]{2,1,0:T(8,128)(2,1)} %bitcast.8, bf16[12,128,1024]{2,1,0:T(8,128)(2,1)} %bitcast.6, bf16[12,128,1024]{2,1,0:T(8,128)(2,1)} %bitcast.7), custom_call_target="tpu_custom_call" | custom-call | tf_op jit(solution)/shard_map/lanczos/pallas_call | solution.py:644
  112.5 2.7 %normalize.1 = (f32[16,128,128]{2,1,0:T(8,128)}, f32[2]{0:T(128)}) custom-call(f32[16,128,128]{2,1,0:T(8,128)} %get-tuple-element.6.applied_in, bf16[16,128,128]{2,1,0:T(8,128)(2,1)} %bitcast.9, f32[3]{0:T(128)} %get-tuple-element.7.terms_in), custom_call_target="tpu_custom_call" | custom-call | tf_op jit(solution)/shard_map/normalize/pallas_call | solution.py:691

commit v6 on v5

--- a/solution.py
+++ b/solution.py
@@ -70,9 +70,8 @@
     state_in,
     left_in,
     right_in,
-    out,
-    coef,
     applied,
+    terms,
     one,
     two,
     state,
@@ -479,17 +478,11 @@
     def folded(value):
         return jnp.sum(value.reshape(-1, 8, 128), axis=0)
 
-    stores = []
-
     @staged
     def finish(u):
         m, i, p = UNITS[u]
         h = lax.rem(x + i, X)
         v, count, rows_here = u % 8, ROWS[m], pl.ds(STARTS[m], ROWS[m])
-        done = (pl.ds(h * 4, 4), rows_here)
-        stores.append(
-            (p, pltpu.make_async_copy(applied.at[done], out.at[done], local_sems.at[H + 13 + u]))
-        )
 
         @pl.when(has_role(p, 1))
         def _():
@@ -515,7 +508,6 @@
             sums = lax.fori_loop(0, 4, piece, (totals[0], totals[1], totals[2]))
             for k in range(3):
                 totals[k] = sums[k]
-            stores[-1][1].start()
 
     @staged
     def turn(k):
@@ -556,12 +548,29 @@
     for name, *numbers in ORDER:
         stages[name](*numbers)
 
+    n_before = len(used)
+
+    def drain():
+        for item in used[:n_before]:
+            if id(item) not in hop_copies:
+                item.wait_send()
+        for p in range(2):
+
+            @pl.when(has_role(p, 1))
+            def _():
+                for (_, _, q), sends in zip(UNITS, hops):
+                    for k in (1, 3) if q == p else (2, 4):
+                        for item in sends[k]:
+                            item.wait_send()
+
     @staged
     def all_sum(phase, values, slots, me, targets):
         slots[me] = values
         sends = [copy(slots.at[me], slots.at[me], target) for target in targets]
         for item in sends:
             item.start()
+        if phase == 0:
+            drain()
         for item in sends:
             item.wait_recv()
         return jnp.sum(slots[...], axis=0)
@@ -581,22 +590,10 @@
     beta = jnp.sqrt(residual_sq + EPSILON)
     scale = 1.0 / (jnp.sqrt(norm_sq) * beta)
     for k, value in enumerate((alpha, beta, scale)):
-        coef[k] = value[0, 0]
+        terms[k : k + 1] = jnp.broadcast_to(value, (1, 128))
     with jax.named_scope("drain"):
-        for item in used:
-            if id(item) not in hop_copies:
-                item.wait_send()
-        for p in range(2):
-
-            @pl.when(has_role(p, 1))
-            def _():
-                for (_, _, q), sends in zip(UNITS, hops):
-                    for k in (1, 3) if q == p else (2, 4):
-                        for item in sends[k]:
-                            item.wait_send()
-                for q, item in stores:
-                    if q == p:
-                        item.wait()
+        for item in used[n_before:]:
+            item.wait_send()
 
 
 def kernel(*refs):
@@ -604,34 +601,24 @@
         functools.partial(step, *refs),
         pltpu.SemaphoreType.DMA((N_SEMS,)),
         pltpu.SemaphoreType.DMA((N_SEMS,)),
-        pltpu.SemaphoreType.DMA((H + 13 + len(UNITS),)),
+        pltpu.SemaphoreType.DMA((H + 13,)),
     )
 
 
-def normalize(applied_in, state_in, terms_in, out, coef, applied, state, result, terms, sems):
-    load_terms = pltpu.make_async_copy(terms_in, terms, sems.at[0])
-    load_terms.start()
-    parts = [pl.ds(4 * k, 4) for k in range(4)]
-    loads, stores = [], []
-    for k, part in enumerate(parts):
-        loads.append(pltpu.make_async_copy(applied_in.at[part], applied.at[part], sems.at[1 + k]))
-        loads.append(pltpu.make_async_copy(state_in.at[part], state.at[part], sems.at[5 + k]))
-        stores.append(pltpu.make_async_copy(result.at[part], out.at[part], sems.at[9 + k]))
-    for item in loads:
-        item.start()
-    load_terms.wait()
-    alpha, beta, scale = (terms[k] for k in range(3))
-    coef[0] = alpha
-    coef[1] = beta
+def normalize(applied, state, terms, out, coef, result, sems):
+    alpha, scale = terms[0:1], terms[2:3]
+    coef[0] = terms[0, 0]
+    coef[1] = terms[1, 0]
+    stores = []
     for k in range(4):
-        loads[2 * k].wait()
-        loads[2 * k + 1].wait()
 
         def rows_of(i, _):
             result[i] = (applied[i] - alpha * state[i].astype(F32)) * scale
             return 0
 
         lax.fori_loop(4 * k, 4 * k + 4, rows_of, 0)
+        part = pl.ds(4 * k, 4)
+        stores.append(pltpu.make_async_copy(result.at[part], out.at[part], sems.at[k]))
         stores[k].start()
     for item in stores:
         item.wait()
@@ -640,17 +627,17 @@
 def body(state, left_env, right_env, site_one, site_two):
     smem = pl.BlockSpec(memory_space=pltpu.SMEM)
     anywhere = pl.BlockSpec(memory_space=pl.ANY)
+    vmem = pl.BlockSpec(memory_space=pltpu.VMEM)
     state = state.reshape(16, 128, 128)
     applied, terms = pl.pallas_call(
         kernel,
         out_shape=(
-            jax.ShapeDtypeStruct((16, 128, 128), F32),
-            jax.ShapeDtypeStruct((3,), F32),
+            pltpu.VMEM((16, 128, 128), F32),
+            pltpu.VMEM((8, 128), F32),
         ),
         in_specs=[anywhere] * 5,
-        out_specs=(anywhere, smem),
+        out_specs=(vmem, vmem),
         scratch_shapes=[
-            pltpu.VMEM((16, 128, 128), F32),
             pltpu.SMEM((3, 2, 2, 3), F32),
             pltpu.SMEM((3, 2, 2, 3), F32),
             pltpu.VMEM((16, 128, 128), BF16),
@@ -678,7 +665,7 @@
             pltpu.VMEM((32, 1, 128), F32),
         ],
         compiler_params=pltpu.CompilerParams(
-            collective_id=0, has_side_effects=True, vmem_limit_bytes=64_000_000
+            collective_id=0, has_side_effects=True, vmem_limit_bytes=58_500_000
         ),
         name="lanczos",
     )(
@@ -694,16 +681,13 @@
             jax.ShapeDtypeStruct((16, 128, 128), F32),
             jax.ShapeDtypeStruct((2,), F32),
         ),
-        in_specs=[anywhere] * 3,
+        in_specs=[vmem, vmem, vmem],
         out_specs=(anywhere, smem),
         scratch_shapes=[
             pltpu.VMEM((16, 128, 128), F32),
-            pltpu.VMEM((16, 128, 128), BF16),
-            pltpu.VMEM((16, 128, 128), F32),
-            pltpu.SMEM((3,), F32),
-            pltpu.SemaphoreType.DMA((13,)),
+            pltpu.SemaphoreType.DMA((4,)),
         ],
-        compiler_params=pltpu.CompilerParams(vmem_limit_bytes=64_000_000),
+        compiler_params=pltpu.CompilerParams(vmem_limit_bytes=8_000_000),
         name="normalize",
     )(applied, state, terms)
     return out.reshape(1, 4, 4, 128, 128), coef

time: 116 us -> 113 us (0.974)
  Pallas kernels: 115 us -> 112 us
where the time goes in v6:
time: 113 us
  Pallas kernels  112 us (99%)
    pallas_call x1, Pallas kernels, body(): pl.pallas_call(kernel, out_shape=(pltpu.VMEM((16, 128, 128), F32), pltpu....  111 us

profile of v6, /device:TPU:1, one launch (start us, length us, event | category | flops | bytes accessed | tf_op | source)
XLA Modules:
  0.0 113.2 jit_solution(12661610797831852596)
XLA Ops:
  0.6 0.0 copy-start
  0.6 110.8 %lanczos.1 = (f32[16,128,128]{2,1,0:T(8,128)S(1)}, f32[8,128]{1,0:T(8,128)S(1)}) custom-call(f32[3,2,2,3]{3,2,1,0:T(2,128)} %bitcast.10, f32[3,2,2,3]{3,2,1,0:T(2,128)} %bitcast.11, bf16[16,128,128]{2,1,0:T(8,128)(2,1)} %bitcast.6, bf16[12,128,1024]{2,1,0:T(8,128)(2,1)} %bitcast.8, bf16[12,128,1024]{2,1,0:T(8,128)(2,1)} %bitcast.9), custom_call_target="tpu_custom_call" | custom-call | tf_op jit(solution)/shard_map/lanczos/pallas_call | solution.py:632
  111.5 0.0 copy-done
  111.5 1.6 %normalize.1 = (f32[16,128,128]{2,1,0:T(8,128)}, f32[2]{0:T(128)}) custom-call(f32[16,128,128]{2,1,0:T(8,128)S(1)} %get-tuple-element.6.applied, bf16[16,128,128]{2,1,0:T(8,128)(2,1)S(1)} %bitcast.7, f32[8,128]{1,0:T(8,128)S(1)} %get-tuple-element.7.terms), custom_call_target="tpu_custom_call" | custom-call | tf_op jit(solution)/shard_map/normalize/pallas_call | solution.py:678
Async XLA Ops:
  0.6 110.8 %copy-start = (bf16[1,4,4,128,128]{4,3,2,1,0:T(8,128)(2,1)S(1)}, bf16[1,4,4,128,128]{4,3,2,1,0:T(8,128)(2,1)}, u32[]{:S(2)}) copy-start(bf16[1,4,4,128,128]{4,3,2,1,0:T(8,128)(2,1)} %param.5) | copy-start | bytes 1572868

commit v7 on v6

--- a/solution.py
+++ b/solution.py
@@ -25,30 +25,30 @@
 
 OWN, TURN, NEAR, REST, BLOCKS, LEFT, DIRECT, FAR, MIX, ENVS, PENVS, RF, FENVS, CON, HOP, FIN = range(16)
 ORDER = (
-    (OWN, 1), (TURN, 0), (OWN, 3), (NEAR, 1), (TURN, 1), (OWN, 0), (TURN, 2), (REST, 1), (TURN, 3), (OWN, 2),
-    (NEAR, 3), (BLOCKS, 1), (LEFT, 1), (LEFT, 9), (DIRECT, 1), (NEAR, 0), (REST, 3), (NEAR, 2), (REST, 2),
-    (ENVS, 0), (ENVS, 1), (FAR, 1), (REST, 0), (ENVS, 2), (BLOCKS, 3), (DIRECT, 9), (LEFT, 3), (DIRECT, 3),
-    (BLOCKS, 2), (LEFT, 2), (DIRECT, 2), (BLOCKS, 0), (LEFT, 0), (DIRECT, 0), (PENVS, 0), (FAR, 2), (FAR, 3),
-    (MIX, 1), (FAR, 0), (ENVS, 3), (PENVS, 1), (LEFT, 8), (RF, 0), (LEFT, 11), (MIX, 2), (LEFT, 10),
-    (DIRECT, 8), (MIX, 3), (MIX, 0), (FAR, 9), (CON, 0), (FAR, 8), (CON, 1), (DIRECT, 11), (CON, 2), (CON, 4),
-    (FAR, 11), (HOP, 0, 2), (DIRECT, 10), (HOP, 1, 2), (FAR, 10), (MIX, 9), (LEFT, 6), (LEFT, 7), (MIX, 8),
-    (LEFT, 5), (HOP, 4, 2), (PENVS, 2), (DIRECT, 6), (LEFT, 4), (MIX, 11), (HOP, 2, 2), (PENVS, 3),
-    (HOP, 1, 3), (HOP, 0, 3), (MIX, 10), (CON, 16), (DIRECT, 5), (CON, 20), (CON, 18), (HOP, 4, 3), (FAR, 6),
-    (RF, 1), (CON, 17), (CON, 5), (HOP, 2, 3), (CON, 19), (CON, 21), (HOP, 16, 2), (FAR, 5), (HOP, 1, 4),
-    (DIRECT, 4), (CON, 3), (HOP, 18, 2), (HOP, 20, 2), (FAR, 4), (FAR, 7), (HOP, 2, 4), (HOP, 17, 2),
-    (HOP, 5, 2), (HOP, 19, 2), (HOP, 0, 4), (HOP, 21, 2), (DIRECT, 7), (FENVS, 0), (HOP, 3, 2), (MIX, 5),
-    (HOP, 4, 4), (MIX, 6), (CON, 22), (MIX, 4), (HOP, 20, 3), (HOP, 17, 3), (CON, 6), (HOP, 5, 3),
-    (HOP, 16, 3), (MIX, 7), (CON, 8), (CON, 13), (CON, 12), (HOP, 21, 3), (HOP, 19, 3), (CON, 10),
-    (HOP, 18, 3), (HOP, 17, 4), (CON, 9), (CON, 14), (HOP, 3, 3), (HOP, 5, 4), (FENVS, 1), (HOP, 13, 2),
-    (HOP, 21, 4), (CON, 11), (HOP, 9, 2), (HOP, 3, 4), (HOP, 22, 2), (HOP, 8, 2), (HOP, 12, 2), (FIN, 1),
-    (CON, 7), (HOP, 11, 2), (CON, 23), (HOP, 10, 2), (HOP, 20, 4), (HOP, 22, 3), (HOP, 7, 2), (HOP, 23, 2),
-    (CON, 15), (HOP, 14, 2), (HOP, 12, 3), (HOP, 6, 2), (HOP, 16, 4), (HOP, 13, 3), (FIN, 4), (HOP, 15, 2),
-    (HOP, 10, 3), (HOP, 14, 3), (HOP, 6, 3), (FIN, 16), (HOP, 9, 3), (HOP, 18, 4), (HOP, 13, 4), (FIN, 2),
-    (FIN, 17), (HOP, 11, 3), (FIN, 0), (HOP, 23, 3), (HOP, 9, 4), (HOP, 7, 3), (HOP, 8, 3), (HOP, 15, 3),
-    (HOP, 11, 4), (HOP, 12, 4), (HOP, 23, 4), (FIN, 20), (FIN, 5), (FIN, 18), (HOP, 7, 4), (HOP, 15, 4),
-    (HOP, 22, 4), (HOP, 10, 4), (HOP, 14, 4), (HOP, 6, 4), (HOP, 8, 4), (FIN, 11), (HOP, 19, 4), (FIN, 22),
-    (FIN, 14), (FIN, 21), (FIN, 12), (FIN, 10), (FIN, 9), (FIN, 3), (FIN, 6), (FIN, 23), (FIN, 7), (FIN, 8),
-    (FIN, 19), (FIN, 13), (FIN, 15),
+    (OWN, 3), (TURN, 0), (OWN, 0), (NEAR, 3), (OWN, 2), (NEAR, 0), (OWN, 1), (REST, 0), (TURN, 1), (REST, 3),
+    (TURN, 2), (BLOCKS, 3), (NEAR, 2), (LEFT, 11), (LEFT, 3), (ENVS, 0), (DIRECT, 3), (TURN, 3), (BLOCKS, 0),
+    (LEFT, 0), (REST, 2), (NEAR, 1), (FAR, 3), (ENVS, 1), (DIRECT, 0), (BLOCKS, 2), (FAR, 0), (LEFT, 2),
+    (REST, 1), (DIRECT, 2), (BLOCKS, 1), (ENVS, 2), (LEFT, 1), (DIRECT, 1), (FAR, 2), (MIX, 0), (PENVS, 0),
+    (FAR, 1), (LEFT, 9), (LEFT, 10), (ENVS, 3), (LEFT, 8), (MIX, 3), (DIRECT, 11), (PENVS, 1), (FAR, 11),
+    (MIX, 2), (DIRECT, 9), (MIX, 1), (DIRECT, 10), (CON, 2), (CON, 1), (DIRECT, 8), (CON, 4), (RF, 0),
+    (CON, 0), (FAR, 8), (HOP, 1, 2), (FAR, 9), (HOP, 2, 2), (FAR, 10), (HOP, 4, 2), (LEFT, 6), (PENVS, 2),
+    (HOP, 0, 2), (LEFT, 4), (LEFT, 7), (HOP, 2, 3), (MIX, 11), (MIX, 8), (LEFT, 5), (HOP, 4, 3), (MIX, 9),
+    (HOP, 1, 3), (PENVS, 3), (RF, 1), (MIX, 10), (CON, 17), (DIRECT, 4), (CON, 18), (CON, 20), (HOP, 2, 4),
+    (HOP, 0, 3), (FAR, 4), (DIRECT, 7), (DIRECT, 6), (CON, 16), (CON, 5), (CON, 3), (FAR, 7), (FAR, 6),
+    (HOP, 17, 2), (CON, 21), (HOP, 1, 4), (HOP, 5, 2), (HOP, 20, 2), (HOP, 18, 2), (FAR, 5), (DIRECT, 5),
+    (CON, 19), (HOP, 0, 4), (HOP, 21, 2), (MIX, 4), (FENVS, 0), (HOP, 16, 2), (HOP, 17, 3), (HOP, 3, 2),
+    (HOP, 20, 3), (MIX, 7), (HOP, 19, 2), (HOP, 4, 4), (HOP, 18, 3), (HOP, 5, 3), (MIX, 6), (CON, 6),
+    (CON, 22), (HOP, 21, 3), (HOP, 17, 4), (MIX, 5), (CON, 11), (CON, 9), (HOP, 16, 3), (HOP, 3, 3),
+    (CON, 12), (CON, 14), (HOP, 5, 4), (HOP, 19, 3), (HOP, 6, 2), (HOP, 21, 4), (CON, 10), (FENVS, 1),
+    (HOP, 9, 2), (CON, 8), (HOP, 3, 4), (HOP, 20, 4), (HOP, 11, 2), (CON, 13), (HOP, 6, 3), (HOP, 12, 2),
+    (HOP, 14, 2), (CON, 7), (CON, 23), (FIN, 2), (HOP, 13, 2), (CON, 15), (HOP, 7, 2), (HOP, 22, 2),
+    (HOP, 16, 4), (HOP, 23, 2), (HOP, 9, 3), (HOP, 8, 2), (HOP, 11, 3), (HOP, 12, 3), (HOP, 10, 2),
+    (HOP, 15, 2), (HOP, 19, 4), (FIN, 0), (HOP, 22, 3), (HOP, 14, 3), (HOP, 18, 4), (HOP, 11, 4),
+    (HOP, 10, 3), (HOP, 6, 4), (FIN, 20), (HOP, 8, 3), (HOP, 23, 3), (HOP, 9, 4), (HOP, 7, 3), (FIN, 17),
+    (FIN, 6), (HOP, 23, 4), (HOP, 15, 3), (FIN, 21), (HOP, 13, 3), (HOP, 22, 4), (HOP, 7, 4), (HOP, 12, 4),
+    (HOP, 15, 4), (FIN, 5), (HOP, 14, 4), (HOP, 13, 4), (FIN, 12), (FIN, 14), (FIN, 22), (FIN, 18),
+    (HOP, 10, 4), (FIN, 3), (FIN, 10), (FIN, 4), (FIN, 19), (HOP, 8, 4), (FIN, 11), (FIN, 16), (FIN, 1),
+    (FIN, 9), (FIN, 23), (FIN, 7), (FIN, 15), (FIN, 13), (FIN, 8),
 )
 
 
@@ -132,12 +132,15 @@
     x_up, x_down = at(dx=1), at(dx=X - 1)
     y_up, y_down = at(dy=1), at(dy=Y - 1)
     z_up, z_down = at(dz=1), at(dz=Z - 1)
-    z_peers = [at(dz=k) for k in range(1, Z)]
+    z_peers = [at(dz=k) for k in (4, 3, 5, 2, 6, 1, 7)]
+    distance = (0, 1, 2, 1)
     xy_peers = [
         at(dx=i, dy=j, core=core)
-        for i in range(X)
-        for j in range(Y)
-        for core in (c, other)
+        for i, j in sorted(
+            ((i, j) for i in range(X) for j in range(Y)),
+            key=lambda ij: -distance[ij[0]] - distance[ij[1]],
+        )
+        for core in (other, c)
         if not (i == 0 and j == 0 and core is c)
     ]
 

time: 113 us -> 112 us (level)
  no operation moved by 1% of the time
where the time goes in v7:
time: 112 us
  Pallas kernels  111 us (99%)
    pallas_call x1, Pallas kernels, body(): pl.pallas_call(kernel, out_shape=(pltpu.VMEM((16, 128, 128), F32), pltpu....  110 us

profile of v7, /device:TPU:1, one launch (start us, length us, event | category | flops | bytes accessed | tf_op | source)
XLA Modules:
  0.0 112.3 jit_solution(4019742804277531330)
XLA Ops:
  0.6 0.0 copy-start
  0.6 109.9 %lanczos.1 = (f32[16,128,128]{2,1,0:T(8,128)S(1)}, f32[8,128]{1,0:T(8,128)S(1)}) custom-call(f32[3,2,2,3]{3,2,1,0:T(2,128)} %bitcast.10, f32[3,2,2,3]{3,2,1,0:T(2,128)} %bitcast.11, bf16[16,128,128]{2,1,0:T(8,128)(2,1)} %bitcast.6, bf16[12,128,1024]{2,1,0:T(8,128)(2,1)} %bitcast.8, bf16[12,128,1024]{2,1,0:T(8,128)(2,1)} %bitcast.9), custom_call_target="tpu_custom_call" | custom-call | tf_op jit(solution)/shard_map/lanczos/pallas_call | solution.py:635
  110.5 0.0 copy-done
  110.5 1.6 %normalize.1 = (f32[16,128,128]{2,1,0:T(8,128)}, f32[2]{0:T(128)}) custom-call(f32[16,128,128]{2,1,0:T(8,128)S(1)} %get-tuple-element.6.applied, bf16[16,128,128]{2,1,0:T(8,128)(2,1)S(1)} %bitcast.7, f32[8,128]{1,0:T(8,128)S(1)} %get-tuple-element.7.terms), custom_call_target="tpu_custom_call" | custom-call | tf_op jit(solution)/shard_map/normalize/pallas_call | solution.py:681
Async XLA Ops:
  0.6 109.9 %copy-start = (bf16[1,4,4,128,128]{4,3,2,1,0:T(8,128)(2,1)S(1)}, bf16[1,4,4,128,128]{4,3,2,1,0:T(8,128)(2,1)}, u32[]{:S(2)}) copy-start(bf16[1,4,4,128,128]{4,3,2,1,0:T(8,128)(2,1)} %param.5) | copy-start | bytes 1572868

commit v8 on v7

--- a/solution.py
+++ b/solution.py
@@ -168,8 +168,7 @@
         )
         for b in range(Z)
     ]
-    for item in load_sites + [load_state, load_left] + local + load_right:
-        item.start()
+    load_state.start()
 
     def fill_pairs():
         for w in range(3):
@@ -184,6 +183,8 @@
 
     with jax.named_scope("entry"):
         load_state.wait()
+        for item in [load_left] + local + load_sites + load_right:
+            item.start()
         pl.semaphore_wait(barrier, len(peers))
 
     g_below = lax.rem(x + X - 1, X) * 2 + c

time: 112 us -> 112 us (level)
  no operation moved by 1% of the time
where the time goes in v8:
time: 112 us
  Pallas kernels  111 us (99%)
    pallas_call x1, Pallas kernels, body(): pl.pallas_call(kernel, out_shape=(pltpu.VMEM((16, 128, 128), F32), pltpu....  110 us

profile of v8, /device:TPU:1, one launch (start us, length us, event | category | flops | bytes accessed | tf_op | source)
XLA Modules:
  0.0 112.3 jit_solution(13553864741170551251)
XLA Ops:
  0.6 0.0 copy-start
  0.6 109.9 %lanczos.1 = (f32[16,128,128]{2,1,0:T(8,128)S(1)}, f32[8,128]{1,0:T(8,128)S(1)}) custom-call(f32[3,2,2,3]{3,2,1,0:T(2,128)} %bitcast.10, f32[3,2,2,3]{3,2,1,0:T(2,128)} %bitcast.11, bf16[16,128,128]{2,1,0:T(8,128)(2,1)} %bitcast.6, bf16[12,128,1024]{2,1,0:T(8,128)(2,1)} %bitcast.8, bf16[12,128,1024]{2,1,0:T(8,128)(2,1)} %bitcast.9), custom_call_target="tpu_custom_call" | custom-call | tf_op jit(solution)/shard_map/lanczos/pallas_call | solution.py:636
  110.5 0.0 copy-done
  110.5 1.6 %normalize.1 = (f32[16,128,128]{2,1,0:T(8,128)}, f32[2]{0:T(128)}) custom-call(f32[16,128,128]{2,1,0:T(8,128)S(1)} %get-tuple-element.6.applied, bf16[16,128,128]{2,1,0:T(8,128)(2,1)S(1)} %bitcast.7, f32[8,128]{1,0:T(8,128)S(1)} %get-tuple-element.7.terms), custom_call_target="tpu_custom_call" | custom-call | tf_op jit(solution)/shard_map/normalize/pallas_call | solution.py:682
Async XLA Ops:
  0.6 109.9 %copy-start = (bf16[1,4,4,128,128]{4,3,2,1,0:T(8,128)(2,1)S(1)}, bf16[1,4,4,128,128]{4,3,2,1,0:T(8,128)(2,1)}, u32[]{:S(2)}) copy-start(bf16[1,4,4,128,128]{4,3,2,1,0:T(8,128)(2,1)} %param.5) | copy-start | bytes 1572868
